TPU v7x, 256 devices: a whole 4x4x8 slice. The times are simulated.
256 devices in a mesh: row: 128 (over z, y, x), width: 2 (over core).
Axes of the slice: x: 4, y: 4, z: 8, core: 2. Of those that a mesh axis runs over, the one named last changes fastest.
Arguments:
- row_numbers: int32 [4096, 2], P('row'), may hold values from 0 to 131071
- item_table: bfloat16 [131072, 64], P('row', 'width'), may hold values from -6 to 6
- dense_part: float32 [4096, 64], P('row', 'width'), may hold values from -6 to 6
- small_ids: int32 [4096], P('row'), may hold values from 0 to 255
- small_table: bfloat16 [256, 64], P('row', 'width'), may hold values from -6 to 6
Outputs:
- features: bfloat16 [4096, 3, 64], P('row', None, 'width')
All inputs are finite; a program needn't handle non-finite values.
Results may differ from a plain program's by a relative error of at most 0.0004.
Values may be sent and summed in bfloat16 or wider, within the bound.
A program may use at most 64 MiB of HBM per device.

v0:
```python
import jax
import jax.numpy as jnp
from jax import lax
from jax.sharding import Mesh
from jax.sharding import PartitionSpec as P

PICKS = 2
ROW = ("row_0", "row_1", "row_2")


def gather_axes(shard, axes, dim):
    whole = shard
    for number in range(len(axes) - 1, -1, -1):
        whole = lax.all_gather(whole, axes[number], axis=dim, tiled=True)
    return whole


def sum_by_axis(product, span, axes):
    so_far = product(jnp.int32(0), span * lax.axis_size(axes))
    for axis in axes:
        so_far = lax.psum_scatter(so_far, axis, scatter_dimension=0, tiled=True)
    return so_far


def own_rows(table_part, wanted, first_row):
    place = wanted - first_row
    inside = (place >= 0) & (place < table_part.shape[0])
    found = jnp.take(table_part, jnp.clip(place, 0, table_part.shape[0] - 1), axis=0).astype(
        jnp.float32
    )
    return jnp.where(inside[..., None], found, 0.0)


def shards(row_numbers, item_table, dense_part, small_ids, small_table):
    big_first = lax.axis_index(ROW) * item_table.shape[0]
    all_ids = gather_axes(row_numbers, ROW, 0)

    def pooled_part(start, count):
        wanted = lax.dynamic_slice_in_dim(all_ids, start, count)
        return jnp.sum(own_rows(item_table, wanted, big_first), axis=1)

    pooled = sum_by_axis(pooled_part, row_numbers.shape[0], ROW) * PICKS ** (-0.5)
    every_row = gather_axes(small_table, ROW, 0)
    small_rows = jnp.take(every_row, small_ids, axis=0).astype(jnp.float32)
    features = jnp.stack([dense_part, pooled, small_rows], axis=1).astype(jnp.bfloat16)
    return features


def solution(mesh):
    torus = Mesh(
        mesh.devices.reshape(8, 4, 4, mesh.shape["width"]), ("row_0", "row_1", "row_2", "width")
    )
    return jax.shard_map(
        shards,
        mesh=torus,
        in_specs=(P(ROW, None), P(ROW, "width"), P(ROW, "width"), P(ROW), P(ROW, "width")),
        out_specs=P(ROW, None, "width"),
        check_vma=False,
    )
```

profile of v0, /device:TPU:1, one launch (start us, length us, event | category | flops | bytes accessed | tf_op | source)
XLA Modules:
  0.0 203.8 jit_solution(2406800571740259842)
XLA Ops:
  6.5 0.0 reduce-scatter.4.cloned.1.call-start
  6.5 8.7 %all-gather = s32[4,32,2]{1,2,0:T(2,128)S(1)} all-gather(s32[1,32,2]{1,2,0:T(2,128)} %bitcast.14), channel_id=1, replica_groups=mesh['row_0'=8,'row_1'=4,'row_2'=4,'width'=2] {'row_2'}, dimensions={0}, use_global_device_ids=true | all-gather | bytes 1280 | tf_op jit(solution)/shard_map/all_gather | solution.py:14
  15.3 0.1 reshape.58
  15.4 8.2 %all_gather.19 = s32[512,2]{0,1:T(2,128)S(1)} all-gather(s32[128,2]{0,1:T(2,128)S(1)} %reshape.58), channel_id=1, replica_groups=mesh['row_0'=8,'row_1'=4,'row_2'=4,'width'=2] {'row_1'}, dimensions={0}, use_global_device_ids=true | all-gather | bytes 5120 | tf_op jit(solution)/shard_map/all_gather | solution.py:14
  23.6 21.7 %all_gather.20 = s32[4096,2]{0,1:T(2,128)S(1)} all-gather(s32[512,2]{0,1:T(2,128)S(1)} %all_gather.19), channel_id=1, replica_groups=mesh['row_0'=8,'row_1'=4,'row_2'=4,'width'=2] {'row_0'}, dimensions={0}, use_global_device_ids=true | all-gather | bytes 36864 | tf_op jit(solution)/shard_map/all_gather | solution.py:14
  45.4 0.1 compare_and_fusion
  45.5 0.0 copy-start
  45.5 0.6 copy.15
  46.1 1.2 reshape.40
  47.3 0.0 copy-done
  47.4 0.2 copy.16
  47.5 0.9 copy.13
  48.4 0.8 copy.14
  49.2 24.0 %gather_fusion = bf16[8192,32]{1,0:T(8,128)(2,1)S(1)} fusion(bf16[1024,32]{1,0:T(8,128)(2,1)S(1)} %copy.16, s32[8192]{0:T(1024)S(1)} %broadcast_clamp_fusion), kind=kCustom, calls=%fused_computation | custom fusion | bytes 1081344 | tf_op jit(solution)/shard_map/jit(_take)/gather | solution.py:28
  73.3 24.5 %select_reduce_fusion = f32[4096,32]{1,0:T(8,128)} fusion(pred[4096,2]{1,0:T(8,128)(4,1)S(1)} %copy.13, bf16[4096,2,32]{2,1,0:T(2,128)(2,1)S(1)} %bitcast.12, pred[4096,2]{1,0:T(8,128)(4,1)S(1)} %copy.14), kind=kLoop, calls=%fused_computation.2 | loop fusion | flops 917504 | bytes 1064960 | tf_op jit(solution)/shard_map/reduce_sum | solution.py:40
  97.8 0.0 copy-start.2
  97.8 0.0 copy-start.3
  97.8 0.0 copy-start.1
  97.8 0.0 reduce-scatter.4.cloned.1.call-update
  97.9 0.0 reduce-scatter.6.cloned.1.call-start
  97.9 0.6 copy-done.2
  98.5 5.2 %all-gather.1 = bf16[4,2,32]{2,1,0:T(2,128)(2,1)S(1)} all-gather(bf16[1,2,32]{2,1,0:T(2,128)(2,1)S(1)} %bitcast.15), channel_id=1, replica_groups=mesh['row_0'=8,'row_1'=4,'row_2'=4,'width'=2] {'row_2'}, dimensions={0}, use_global_device_ids=true | all-gather | bytes 640 | tf_op jit(solution)/shard_map/all_gather | solution.py:14
  103.7 8.9 %all_gather.22 = bf16[32,32]{1,0:T(8,128)(2,1)S(1)} all-gather(bf16[8,32]{1,0:T(8,128)(2,1)S(1)} %bitcast.13), channel_id=1, replica_groups=mesh['row_0'=8,'row_1'=4,'row_2'=4,'width'=2] {'row_1'}, dimensions={0}, use_global_device_ids=true | all-gather | bytes 2560 | tf_op jit(solution)/shard_map/all_gather | solution.py:14
  112.6 19.5 %all_gather.23 = bf16[256,32]{1,0:T(8,128)(2,1)S(1)} all-gather(bf16[32,32]{1,0:T(8,128)(2,1)S(1)} %all_gather.22), channel_id=1, replica_groups=mesh['row_0'=8,'row_1'=4,'row_2'=4,'width'=2] {'row_0'}, dimensions={0}, use_global_device_ids=true | all-gather | bytes 18432 | tf_op jit(solution)/shard_map/all_gather | solution.py:14
  132.1 0.0 copy-done.3
  132.2 0.6 gather_fusion.1
  132.8 0.0 copy-done.1
  132.8 8.2 %reduce-scatter.4.cloned.1.call-done = f32[512,32]{1,0:T(8,128)} async-done(((f32[4096,32]{1,0:T(8,128)}), f32[512,32]{1,0:T(8,128)}) %reduce-scatter.4.cloned.1.call-update) | async-done | bytes 65552 | tf_op jit(solution)/shard_map/reduce_scatter | solution.py:21
  141.0 0.0 reduce-scatter.6.cloned.1.call-update
  141.0 0.0 reduce-scatter.8.cloned.1.call-start
  141.0 29.5 %reduce-scatter.6.cloned.1.call-done = f32[128,32]{1,0:T(8,128)} async-done(((f32[512,32]{1,0:T(8,128)}), f32[128,32]{1,0:T(8,128)}) %reduce-scatter.6.cloned.1.call-update) | async-done | bytes 16400 | tf_op jit(solution)/shard_map/reduce_scatter | solution.py:21
  170.6 0.0 reduce-scatter.8.cloned.1.call-update
  170.6 0.1 bitcast_select_fusion
  170.7 25.3 %reduce-scatter.8.cloned.1.call-done = f32[32,32]{1,0:T(8,128)} async-done(((f32[128,32]{1,0:T(8,128)}), f32[32,32]{1,0:T(8,128)}) %reduce-scatter.8.cloned.1.call-update) | async-done | bytes 4112 | tf_op jit(solution)/shard_map/reduce_scatter | solution.py:21
  195.9 0.7 fusion
  196.6 0.6 pad_maximum_fusion
  (6 shorter events, 0.0 us)
Async XLA Ops:
  6.5 134.4 %reduce-scatter.4.cloned.1.call-start = ((), (), s32[]{:S(2)}) async-start(), calls=%async_computation.3 | async-start | bytes 2359296 | tf_op jit(solution)/shard_map/reduce_scatter | solution.py:21
  45.5 1.9 copy-start
  97.8 0.7 copy-start.2
  97.8 34.3 %copy-start.3 = (s32[32]{0:T(128)S(1)}, s32[32]{0:T(128)}, u32[]{:S(2)}) copy-start(s32[32]{0:T(128)} %param.8) | copy-start | bytes 388
  97.8 34.9 %copy-start.1 = (f32[32,32]{1,0:T(8,128)S(1)}, f32[32,32]{1,0:T(8,128)}, u32[]{:S(2)}) copy-start(f32[32,32]{1,0:T(8,128)} %param.7) | copy-start | bytes 12292
  97.9 72.7 %reduce-scatter.6.cloned.1.call-start = ((), (), s32[]{:S(2)}) async-start(), calls=%async_computation.4 | async-start | bytes 327680 | tf_op jit(solution)/shard_map/reduce_scatter | solution.py:21
  141.0 54.9 %reduce-scatter.8.cloned.1.call-start = ((), (), s32[]{:S(2)}) async-start(), calls=%async_computation.5 | async-start | bytes 81920 | tf_op jit(solution)/shard_map/reduce_scatter | solution.py:21
Sparse Core Ops, SparseCore 0:
  98.0 42.9 reduce-scatter.3
  143.5 27.0 reduce-scatter.5
  173.1 22.8 reduce-scatter.7
where the time goes:
time: 205 us; the launch traced here: 204 us
  blocking collectives  72.4 us (35%)
  waiting for transfers between devices  63 us (31%)
  local copies, waits for them, and re-layouts  29 us (14%)
  other arithmetic  26.1 us (13%)
  between operations  13.2 us (6%)
    all_gather x6, blocking collectives, gather_axes(): whole = lax.all_gather(whole, axes[number], axis=dim, tiled=True)  72.4 us
    reduce_scatter x3, waiting for transfers between devices, sum_by_axis(): so_far = lax.psum_scatter(so_far, axis, scatter_dimension=0, tiled=True)  63 us
    reduce_sum x1, other arithmetic, pooled_part(): return jnp.sum(own_rows(item_table, wanted, big_first), axis=1)  24.5 us
    gather x1, local copies, waits for them, and re-layouts, own_rows(): jnp.take(table_part, jnp.clip(place, 0, table_part.shape[0] - 1), axis=0)  24 us
  transfers between devices with their start and end apart: 3, of which 3 were waited for; matrix products, arithmetic and copies ran while one was open for 0% of the time, Pallas kernels for 0%

commit v1 on v0

v1 whole, which is shorter than its diff:
```python
import functools

import jax
import jax.numpy as jnp
from jax import lax
from jax.experimental import pallas as pl
from jax.experimental.pallas import tpu as pltpu
from jax.sharding import Mesh
from jax.sharding import PartitionSpec as P

ROW = ("row_0", "row_1", "row_2")
NZ, NY, NX = 8, 4, 4
MESH = pl.DeviceIdType.MESH
OFFSETS = sorted(
    ((kz, ky) for kz in range(NZ) for ky in range(NY)),
    key=lambda k: (min(k[0], NZ - k[0]) + min(k[1], NY - k[1]), k),
)
SLOT = {k: i for i, k in enumerate(OFFSETS)}
BACK = [SLOT[(-kz % NZ, -ky % NY)] for kz, ky in OFFSETS]
PEERS = len(OFFSETS)
ROWS = 1024
LOW = 256
HIGH = ROWS // LOW
EX = 32
F = 32


def kernel(
    ids_hbm, table_hbm, dense_hbm, sid_hbm, small_hbm, out_ref,
    ids_in, dense, sid, small_in, msg, ids, tab, send, recv, small,
    local_sem, tab_send, tab_recv, ids_send, ids_recv, row_send, row_recv,
    sx_send, sx_recv, sp_send, sp_recv,
):
    z, y, x, w = (lax.axis_index(name) for name in (*ROW, "width"))

    def plane_peer(slot):
        kz, ky = OFFSETS[slot]
        return (lax.rem(z + kz, NZ), lax.rem(y + ky, NY), x, w)

    def x_peer(k):
        return (z, y, lax.rem(x + k, NX), w)

    barrier = pltpu.get_barrier_semaphore()
    for k in range(1, NX):
        pl.semaphore_signal(barrier, inc=1, device_id=x_peer(k), device_id_type=MESH)
    for slot in range(PEERS - 1, 0, -1):
        pl.semaphore_signal(barrier, inc=1, device_id=plane_peer(slot), device_id_type=MESH)

    fetches = [
        pltpu.make_async_copy(src, dst, local_sem.at[i])
        for i, (src, dst) in enumerate(
            (
                (ids_hbm, ids_in), (small_hbm, small_in), (table_hbm, tab.at[0]),
                (sid_hbm, sid), (dense_hbm, dense),
            )
        )
    ]
    for fetch in fetches:
        fetch.start()

    group = z * NY + y
    fetches[0].wait()
    pair = ids_in[...]
    line = jnp.concatenate([pair[0:1], pair[1:2], pair[0:1], pair[1:2]], axis=1)
    msg[...] = line
    ids[0:1, :] = line
    fetches[1].wait()
    my_small = small.at[pl.ds(group * 8 + x * 2, 2)]
    my_small[...] = small_in[...].astype(jnp.float32)
    fetches[2].wait()

    pl.semaphore_wait(barrier, PEERS - 1 + NX - 1)

    def remote(src, dst, s, r, peer):
        return pltpu.make_async_remote_copy(
            src_ref=src, dst_ref=dst, send_sem=s, recv_sem=r, device_id=peer, device_id_type=MESH
        )

    id_copies = {
        slot: remote(
            msg, ids.at[pl.ds(BACK[slot], 1)], ids_send.at[slot], ids_recv.at[BACK[slot]],
            plane_peer(slot),
        )
        for slot in range(1, PEERS)
    }
    sx_copies = [
        remote(my_small, my_small, sx_send.at[k], sx_recv.at[NX - k], x_peer(k))
        for k in range(1, NX)
    ]
    tab_copies = [
        remote(tab.at[0], tab.at[NX - k], tab_send.at[k], tab_recv.at[NX - k], x_peer(k))
        for k in range(1, NX)
    ]
    for slot in range(PEERS - 1, 0, -1):
        id_copies[slot].start()
    for copy in sx_copies:
        copy.start()
    for copy in tab_copies:
        copy.start()

    for copy in sx_copies:
        copy.wait_recv()
    my_eight = small.at[pl.ds(pl.multiple_of(group * 8, 8), 8)]
    sp_copies = [
        remote(my_eight, my_eight, sp_send.at[slot], sp_recv.at[BACK[slot]], plane_peer(slot))
        for slot in range(1, PEERS)
    ]
    for copy in reversed(sp_copies):
        copy.start()

    fetches[3].wait()
    fetches[4].wait()
    out_ref[0] = dense[...].astype(jnp.bfloat16)

    for copy in tab_copies:
        copy.wait_recv()
    lhs = jnp.concatenate(
        [tab[j, :, b * LOW : (b + 1) * LOW] for j in range(NX) for b in range(HIGH)], axis=0
    )
    lane = lax.broadcasted_iota(jnp.int32, (1, 128), 1)
    low_half = lane < 64
    low_half16 = lax.broadcasted_iota(jnp.int32, (16, 128), 1) < 64
    base = group * (NX * ROWS)
    low_rows = lax.broadcasted_iota(jnp.int32, (LOW, 4 * 64), 0)

    row_copies = []
    for first in range(0, PEERS, 4):
        slots = range(first, first + 4)
        for slot in slots:
            if slot:
                id_copies[BACK[slot]].wait_recv()
        lines = [ids[slot : slot + 1, :] for slot in slots]
        wanted = jnp.concatenate(
            [jnp.where(low_half, lines[0], lines[1]), jnp.where(low_half, lines[2], lines[3])],
            axis=1,
        ) - base
        low = wanted & (LOW - 1)
        high = wanted >> 8
        one_hot = jnp.where(low_rows == low, 1.0, 0.0).astype(jnp.bfloat16)
        found = jnp.dot(lhs, one_hot, preferred_element_type=jnp.float32)
        rows = jnp.zeros((F, 4 * 64), jnp.float32)
        for j in range(NX):
            owner = lax.rem(x + j, NX)
            for b in range(HIGH):
                at = (j * HIGH + b) * F
                rows = jnp.where(high == owner * HIGH + b, found[at : at + F], rows)
        for half in range(2):
            part = rows[:, half * 128 : (half + 1) * 128]
            upper, lower = part[:16], part[16:]
            turned_upper = pltpu.roll(upper, 64, 1)
            turned_lower = pltpu.roll(lower, 64, 1)
            even = jnp.where(low_half16, upper, turned_lower).astype(jnp.bfloat16)
            odd = jnp.where(low_half16, turned_upper, lower).astype(jnp.bfloat16)
            for slot, block in ((first + 2 * half, even), (first + 2 * half + 1, odd)):
                if slot == 0:
                    recv[0] = block
                    continue
                send[slot] = block
                copy = remote(
                    send.at[slot], recv.at[BACK[slot]], row_send.at[slot],
                    row_recv.at[BACK[slot]], plane_peer(slot),
                )
                copy.start()
                row_copies.append(copy)

    for copy in sp_copies:
        copy.wait_recv()
    small_hot = jnp.where(
        lax.broadcasted_iota(jnp.int32, (256, EX), 0) == sid[...], 1.0, 0.0
    ).astype(jnp.bfloat16)
    out_ref[2] = lax.dot_general(
        small_hot, small[...].astype(jnp.bfloat16), (((0,), (0,)), ((), ())),
        preferred_element_type=jnp.float32,
    ).astype(jnp.bfloat16)

    for copy in tab_copies + sx_copies + sp_copies + list(id_copies.values()):
        copy.wait_send()
    for copy in row_copies:
        copy.wait_send()
    for copy in row_copies:
        copy.wait_recv()

    total = recv[0].astype(jnp.float32)
    for slot in range(1, PEERS):
        total = total + recv[slot].astype(jnp.float32)
    both = jnp.concatenate(
        [jnp.where(low_half16, total, 0.0), jnp.where(low_half16, 0.0, total)], axis=0
    ).astype(jnp.bfloat16)
    example = lax.broadcasted_iota(jnp.int32, (EX, 128), 0)
    spot = lax.broadcasted_iota(jnp.int32, (EX, 128), 1)
    picks = jnp.where((spot & (EX - 1)) == example, 1.0, 0.0).astype(jnp.bfloat16)
    pooled = lax.dot_general(
        picks, both, (((1,), (1,)), ((), ())), preferred_element_type=jnp.float32
    )
    out_ref[1] = (pooled * 2 ** (-0.5)).astype(jnp.bfloat16)


def shards(row_numbers, item_table, dense_part, small_ids, small_table):
    any_space = pl.BlockSpec(memory_space=pl.ANY)
    dma = pltpu.SemaphoreType.DMA
    parts = pl.pallas_call(
        kernel,
        out_shape=jax.ShapeDtypeStruct((3, EX, F), jnp.bfloat16),
        in_specs=[any_space] * 5,
        out_specs=pl.BlockSpec(memory_space=pltpu.VMEM),
        scratch_shapes=[
            pltpu.VMEM((2, EX), jnp.int32),
            pltpu.VMEM((EX, F), jnp.float32),
            pltpu.VMEM((1, EX), jnp.int32),
            pltpu.VMEM((2, F), jnp.bfloat16),
            pltpu.VMEM((1, 128), jnp.int32),
            pltpu.VMEM((PEERS, 128), jnp.int32),
            pltpu.VMEM((NX, F, ROWS), jnp.bfloat16),
            pltpu.VMEM((PEERS, 16, 128), jnp.bfloat16),
            pltpu.VMEM((PEERS, 16, 128), jnp.bfloat16),
            pltpu.VMEM((256, F), jnp.float32),
            dma((5,)), dma((NX,)), dma((NX,)), dma((PEERS,)), dma((PEERS,)),
            dma((PEERS,)), dma((PEERS,)), dma((NX,)), dma((NX,)), dma((PEERS,)), dma((PEERS,)),
        ],
        compiler_params=pltpu.CompilerParams(collective_id=0, has_side_effects=True),
    )(row_numbers.T, item_table.T, dense_part, small_ids.reshape(1, EX), small_table)
    return parts.transpose(1, 0, 2)


def solution(mesh):
    torus = Mesh(mesh.devices.reshape(NZ, NY, NX, 2), (*ROW, "width"))
    return jax.shard_map(
        shards,
        mesh=torus,
        in_specs=(P(ROW, None), P(ROW, "width"), P(ROW, "width"), P(ROW), P(ROW, "width")),
        out_specs=P(ROW, None, "width"),
        check_vma=False,
    )
```

time: 205 us -> 27.1 us (0.13)
  blocking collectives: 72.4 us -> 0 us
  waiting for transfers between devices: 63 us -> 0 us
  local copies, waits for them, and re-layouts: 29 us -> 1.35 us
  other arithmetic: 26.1 us -> 0 us
  Pallas kernels: 0 us -> 25.6 us
  between operations: 13.2 us -> 0.01 us
    all_gather x6 -> x0, blocking collectives: 72.4 us -> none  [gather_axes(): whole = lax.all_gather(whole, axes[number], axis=dim, tiled=True)]
    reduce_scatter x3 -> x0, waiting for transfers between devices: 63 us -> none  [sum_by_axis(): so_far = lax.psum_scatter(so_far, axis, scatter_dimension=0, tiled=True)]
    pallas_call x0 -> x1, Pallas kernels: none -> 25.6 us  [shards(): pl.pallas_call(kernel, out_shape=jax.ShapeDtypeStruct((3, EX, F), jnp.bfl...]
    gather x2 -> x0, local copies, waits for them, and re-layouts: 24.6 us -> none  [the longest x1 24 us: own_rows(): jnp.take(table_part, jnp.clip(place, 0, table_part.shape[0] - 1), axis=0)]
    reduce_sum x1 -> x0, other arithmetic: 24.5 us -> none  [pooled_part(): return jnp.sum(own_rows(item_table, wanted, big_first), axis=1)]
  transfers between devices with their start and end apart: 3 -> 0, of which waited for: 3 -> 0; matrix products, arithmetic and copies ran while one was open for 0% -> 0% of each run, Pallas kernels for 0% -> 0%
where the time goes in v1:
time: 27.1 us; the launch traced here: 26.9 us
  Pallas kernels  25.6 us (94%)
  local copies, waits for them, and re-layouts  1.35 us (5%)
    pallas_call x1, Pallas kernels, shards(): pl.pallas_call(kernel, out_shape=jax.ShapeDtypeStruct((3, EX, F), jnp.bfl...  25.6 us
    unnamed x1, local copies, waits for them, and re-layouts  1.35 us

profile of v1, /device:TPU:1, one launch (start us, length us, event | category | flops | bytes accessed | tf_op | source)
XLA Modules:
  0.0 26.9 jit_solution(12813301100425425062)
XLA Ops:
  0.0 25.6 %shard_map.55 = bf16[3,32,32]{2,1,0:T(8,128)(2,1)} custom-call(s32[2,32]{1,0:T(2,128)} %bitcast.6, bf16[32,1024]{1,0:T(8,128)(2,1)} %bitcast.5, f32[32,32]{1,0:T(8,128)} %dense_hbm.1, s32[1,32]{1,0:T(1,128)} %bitcast.7, bf16[2,32]{1,0:T(2,128)(2,1)} %small_hbm.1), custom_call_target="tpu_custom_call" | custom-call | tf_op jit(solution)/shard_map/pallas_call | solution.py:201
  25.6 1.3 %copy.7 = bf16[32,3,32]{2,0,1:T(8,128)(2,1)} copy(bf16[32,3,32]{2,0,1:T(8,128)(2,1)} %bitcast.4) | data formatting | bytes 12288

commit v2 on v1

v2 whole, which is shorter than its diff:
```python
import functools

import jax
import jax.numpy as jnp
from jax import lax
from jax.experimental import pallas as pl
from jax.experimental.pallas import tpu as pltpu
from jax.sharding import Mesh
from jax.sharding import PartitionSpec as P

ROW = ("row_0", "row_1", "row_2")
NZ, NY, NX = 8, 4, 4
MESH = pl.DeviceIdType.MESH
OFFSETS = sorted(
    ((kz, ky) for kz in range(NZ) for ky in range(NY)),
    key=lambda k: (min(k[0], NZ - k[0]) + min(k[1], NY - k[1]), k),
)
SLOT = {k: i for i, k in enumerate(OFFSETS)}
BACK = [SLOT[(-kz % NZ, -ky % NY)] for kz, ky in OFFSETS]
PEERS = len(OFFSETS)
ROWS = 1024
LOW = 256
HIGH = ROWS // LOW
EX = 32
F = 32


CHUNKS = 4
PER = PEERS // CHUNKS
WIDE = PER * 64


def kernel(
    ids_hbm, table_hbm, dense_hbm, sid_hbm, small_hbm, out_ref,
    ids_in, dense, sid, small_in, msg, ids, tab, hot, highs, sums, send, recv, small,
    local_sem, tab_send, tab_recv, ids_send, ids_recv, row_send, row_recv,
    sx_send, sx_recv, sp_send, sp_recv,
):
    z, y, x, w = (lax.axis_index(name) for name in (*ROW, "width"))

    def plane_peer(slot):
        kz, ky = OFFSETS[slot]
        return (lax.rem(z + kz, NZ), lax.rem(y + ky, NY), x, w)

    def x_peer(k):
        return (z, y, lax.rem(x + k, NX), w)

    barrier = pltpu.get_barrier_semaphore()
    for slot in range(PEERS - 1, 0, -1):
        pl.semaphore_signal(barrier, inc=1, device_id=plane_peer(slot), device_id_type=MESH)
    for k in range(1, NX):
        pl.semaphore_signal(barrier, inc=1, device_id=x_peer(k), device_id_type=MESH)

    fetches = [
        pltpu.make_async_copy(src, dst, local_sem.at[i])
        for i, (src, dst) in enumerate(
            (
                (ids_hbm, ids_in), (small_hbm, small_in), (table_hbm, tab.at[0]),
                (sid_hbm, sid), (dense_hbm, dense),
            )
        )
    ]
    for fetch in fetches:
        fetch.start()

    group = z * NY + y
    fetches[0].wait()
    pair = ids_in[...]
    line = jnp.concatenate([pair[0:1], pair[1:2], pair[0:1], pair[1:2]], axis=1)
    msg[...] = line
    ids[0:1, :] = line
    fetches[1].wait()
    my_small = small.at[x, pl.ds(group * 2, 2)]
    my_small[...] = small_in[...].astype(jnp.float32)
    fetches[2].wait()
    fetches[3].wait()
    fetches[4].wait()
    out_ref[0] = dense[...].astype(jnp.bfloat16)

    pl.semaphore_wait(barrier, PEERS - 1 + NX - 1)

    def remote(src, dst, s, r, peer):
        return pltpu.make_async_remote_copy(
            src_ref=src, dst_ref=dst, send_sem=s, recv_sem=r, device_id=peer, device_id_type=MESH
        )

    id_copies = {
        slot: remote(
            msg, ids.at[pl.ds(BACK[slot], 1)], ids_send.at[slot], ids_recv.at[BACK[slot]],
            plane_peer(slot),
        )
        for slot in range(1, PEERS)
    }
    sp_copies = {
        slot: remote(
            my_small, my_small, sp_send.at[slot], sp_recv.at[BACK[slot]], plane_peer(slot)
        )
        for slot in range(1, PEERS)
    }
    tab_copies = [
        remote(tab.at[0], tab.at[NX - k], tab_send.at[k], tab_recv.at[NX - k], x_peer(k))
        for k in range(1, NX)
    ]
    for copy in tab_copies:
        copy.start()
    for slot in range(PEERS - 1, 0, -1):
        id_copies[slot].start()
    for slot in range(PEERS - 1, 0, -1):
        sp_copies[slot].start()

    lane = lax.broadcasted_iota(jnp.int32, (1, 128), 1)
    low_half = lane < 64
    low_half16 = lax.broadcasted_iota(jnp.int32, (16, 128), 1) < 64
    base = group * (NX * ROWS)
    low_rows = lax.broadcasted_iota(jnp.int32, (LOW, WIDE), 0)

    def look_up(chunk, j, rows):
        lhs = jnp.concatenate(
            [tab[j, :, b * LOW : (b + 1) * LOW] for b in range(HIGH)], axis=0
        )
        found = jnp.dot(lhs, hot[chunk], preferred_element_type=jnp.float32)
        high = highs[chunk]
        owner = lax.rem(x + j, NX)
        for b in range(HIGH):
            rows = jnp.where(high == owner * HIGH + b, found[b * F : (b + 1) * F], rows)
        return rows

    for chunk in range(CHUNKS):
        slots = range(chunk * PER, (chunk + 1) * PER)
        for slot in slots:
            if slot:
                id_copies[BACK[slot]].wait_recv()
        lines = [ids[slot : slot + 1, :] for slot in slots]
        wanted = jnp.concatenate(
            [jnp.where(low_half, a, b) for a, b in zip(lines[::2], lines[1::2])], axis=1
        ) - base
        highs[chunk] = wanted >> 8
        hot[chunk] = jnp.where(low_rows == (wanted & (LOW - 1)), 1.0, 0.0).astype(jnp.bfloat16)
        sums[chunk] = look_up(chunk, 0, jnp.zeros((F, WIDE), jnp.float32))

    for slot in range(1, PEERS):
        sp_copies[slot].wait_recv()
    sx_copies = [
        remote(small.at[x], small.at[x], sx_send.at[k], sx_recv.at[NX - k], x_peer(k))
        for k in range(1, NX)
    ]
    for copy in sx_copies:
        copy.start()

    for j in (1, 3):
        tab_copies[NX - j - 1].wait_recv()
        for chunk in range(CHUNKS):
            sums[chunk] = look_up(chunk, j, sums[chunk])
    tab_copies[1].wait_recv()
    row_copies = []
    for chunk in range(CHUNKS - 1, -1, -1):
        rows = look_up(chunk, 2, sums[chunk])
        for half in range(PER // 2):
            part = rows[:, half * 128 : (half + 1) * 128]
            upper, lower = part[:16], part[16:]
            turned_upper = pltpu.roll(upper, 64, 1)
            turned_lower = pltpu.roll(lower, 64, 1)
            even = jnp.where(low_half16, upper, turned_lower).astype(jnp.bfloat16)
            odd = jnp.where(low_half16, turned_upper, lower).astype(jnp.bfloat16)
            slot = chunk * PER + 2 * half
            if slot:
                send[slot] = even
            else:
                recv[0] = even
            send[slot + 1] = odd
        for slot in range((chunk + 1) * PER - 1, max(chunk * PER, 1) - 1, -1):
            copy = remote(
                send.at[slot], recv.at[BACK[slot]], row_send.at[slot],
                row_recv.at[BACK[slot]], plane_peer(slot),
            )
            copy.start()
            row_copies.append(copy)

    for copy in sx_copies:
        copy.wait_recv()
    wanted = sid[...]
    place = ((wanted >> 1) & (NX - 1)) * 64 + (wanted >> 3) * 2 + (wanted & 1)
    small_hot = jnp.where(
        lax.broadcasted_iota(jnp.int32, (256, EX), 0) == place, 1.0, 0.0
    ).astype(jnp.bfloat16)
    small_rows = jnp.concatenate([small[k] for k in range(NX)], axis=0).astype(jnp.bfloat16)
    out_ref[2] = lax.dot_general(
        small_hot, small_rows, (((0,), (0,)), ((), ())), preferred_element_type=jnp.float32
    ).astype(jnp.bfloat16)

    for copy in tab_copies + sx_copies + list(sp_copies.values()) + list(id_copies.values()):
        copy.wait_send()
    for copy in row_copies:
        copy.wait_send()
    for copy in row_copies:
        copy.wait_recv()

    total = recv[0].astype(jnp.float32)
    for slot in range(1, PEERS):
        total = total + recv[slot].astype(jnp.float32)
    both = jnp.concatenate(
        [jnp.where(low_half16, total, 0.0), jnp.where(low_half16, 0.0, total)], axis=0
    ).astype(jnp.bfloat16)
    example = lax.broadcasted_iota(jnp.int32, (EX, 128), 0)
    spot = lax.broadcasted_iota(jnp.int32, (EX, 128), 1)
    picks = jnp.where((spot & (EX - 1)) == example, 1.0, 0.0).astype(jnp.bfloat16)
    pooled = lax.dot_general(
        picks, both, (((1,), (1,)), ((), ())), preferred_element_type=jnp.float32
    )
    out_ref[1] = (pooled * 2 ** (-0.5)).astype(jnp.bfloat16)


def shards(row_numbers, item_table, dense_part, small_ids, small_table):
    dma = pltpu.SemaphoreType.DMA
    parts = pl.pallas_call(
        kernel,
        out_shape=jax.ShapeDtypeStruct((3, EX, F), jnp.bfloat16),
        in_specs=[pl.BlockSpec(memory_space=pltpu.HBM)] * 5,
        out_specs=pl.BlockSpec(memory_space=pltpu.VMEM),
        scratch_shapes=[
            pltpu.VMEM((2, EX), jnp.int32),
            pltpu.VMEM((EX, F), jnp.float32),
            pltpu.VMEM((1, EX), jnp.int32),
            pltpu.VMEM((2, F), jnp.bfloat16),
            pltpu.VMEM((1, 128), jnp.int32),
            pltpu.VMEM((PEERS, 128), jnp.int32),
            pltpu.VMEM((NX, F, ROWS), jnp.bfloat16),
            pltpu.VMEM((CHUNKS, LOW, WIDE), jnp.bfloat16),
            pltpu.VMEM((CHUNKS, 1, WIDE), jnp.int32),
            pltpu.VMEM((CHUNKS, F, WIDE), jnp.float32),
            pltpu.VMEM((PEERS, 16, 128), jnp.bfloat16),
            pltpu.VMEM((PEERS, 16, 128), jnp.bfloat16),
            pltpu.VMEM((NX, 2 * PEERS, F), jnp.float32),
            dma((5,)), dma((NX,)), dma((NX,)), dma((PEERS,)), dma((PEERS,)),
            dma((PEERS,)), dma((PEERS,)), dma((NX,)), dma((NX,)), dma((PEERS,)), dma((PEERS,)),
        ],
        compiler_params=pltpu.CompilerParams(
            collective_id=0, has_side_effects=True, vmem_limit_bytes=16 * 2**20
        ),
    )(row_numbers.T, item_table.T, dense_part, small_ids.reshape(1, EX), small_table)
    return parts.transpose(1, 0, 2)


def solution(mesh):
    torus = Mesh(mesh.devices.reshape(NZ, NY, NX, 2), (*ROW, "width"))
    return jax.shard_map(
        shards,
        mesh=torus,
        in_specs=(P(ROW, None), P(ROW, "width"), P(ROW, "width"), P(ROW), P(ROW, "width")),
        out_specs=P(ROW, None, "width"),
        check_vma=False,
    )
```

time: 27.1 us -> 27.8 us (1.026)
  the two profiles are of different devices: /device:TPU:1 before, /device:TPU:2 now
where the time goes in v2:
time: 27.8 us; the launch traced here: 27.6 us
  Pallas kernels  24.7 us (89%)
  local copies, waits for them, and re-layouts  2.86 us (10%)
    pallas_call x1, Pallas kernels, shards(): pl.pallas_call(kernel, out_shape=jax.ShapeDtypeStruct((3, EX, F), jnp.bfl...  24.7 us
    unnamed x11, local copies, waits for them, and re-layouts  2.86 us

profile of v2, /device:TPU:2, one launch (start us, length us, event | category | flops | bytes accessed | tf_op | source)
XLA Modules:
  0.0 27.6 jit_solution(9263954885022343366)
XLA Ops:
  0.0 0.0 copy-start.4
  0.0 0.0 copy-start.2
  0.0 0.0 copy-start.3
  0.0 0.6 %copy-done.4 = bf16[2,32]{1,0:T(2,128)(2,1)S(1)} copy-done((bf16[2,32]{1,0:T(2,128)(2,1)S(1)}, bf16[2,32]{1,0:T(2,128)(2,1)}, u32[]{:S(2)}) %copy-start.4) | copy-done | bytes 152
  0.7 0.0 copy-done.2
  0.7 0.0 copy-done.3
  0.7 0.0 copy-start
  0.7 0.8 %copy-done = bf16[1024,32]{0,1:T(8,128)(2,1)S(1)} copy-done((bf16[1024,32]{0,1:T(8,128)(2,1)S(1)}, bf16[1024,32]{0,1:T(8,128)(2,1)}, u32[]{:S(2)}) %copy-start) | copy-done | bytes 65560
  1.5 0.0 copy-start.1
  1.5 0.7 %copy-done.1 = f32[32,32]{1,0:T(8,128)S(1)} copy-done((f32[32,32]{1,0:T(8,128)S(1)}, f32[32,32]{1,0:T(8,128)}, u32[]{:S(2)}) %copy-start.1) | copy-done | bytes 4120
  2.3 24.7 %shard_map.55 = bf16[3,32,32]{2,1,0:T(8,128)(2,1)S(1)} custom-call(s32[2,32]{1,0:T(2,128)S(1)} %bitcast.6, bf16[32,1024]{1,0:T(8,128)(2,1)S(1)} %bitcast.5, f32[32,32]{1,0:T(8,128)S(1)} %copy-done.1, s32[1,32]{1,0:T(1,128)S(1)} %bitcast.7, bf16[2,32]{1,0:T(2,128)(2,1)S(1)} %copy-done.4), custom_call_target="tpu_custom_call" | custom-call | tf_op jit(solution)/shard_map/pallas_call | solution.py:215
  27.0 0.6 %copy.7 = bf16[32,3,32]{2,0,1:T(8,128)(2,1)} copy(bf16[32,3,32]{2,0,1:T(8,128)(2,1)S(1)} %bitcast.4) | data formatting | bytes 12288
Async XLA Ops:
  0.0 0.7 %copy-start.4 = (bf16[2,32]{1,0:T(2,128)(2,1)S(1)}, bf16[2,32]{1,0:T(2,128)(2,1)}, u32[]{:S(2)}) copy-start(bf16[2,32]{1,0:T(2,128)(2,1)} %small_hbm.1) | copy-start | bytes 388
  0.0 0.7 %copy-start.2 = (s32[32,2]{0,1:T(2,128)S(1)}, s32[32,2]{0,1:T(2,128)}, u32[]{:S(2)}) copy-start(s32[32,2]{0,1:T(2,128)} %param.5) | copy-start | bytes 772
  0.0 0.7 %copy-start.3 = (s32[32]{0:T(128)S(1)}, s32[32]{0:T(128)}, u32[]{:S(2)}) copy-start(s32[32]{0:T(128)} %param.8) | copy-start | bytes 388
  0.7 0.8 %copy-start = (bf16[1024,32]{0,1:T(8,128)(2,1)S(1)}, bf16[1024,32]{0,1:T(8,128)(2,1)}, u32[]{:S(2)}) copy-start(bf16[1024,32]{0,1:T(8,128)(2,1)} %param.6) | copy-start | bytes 196612
  1.5 0.7 %copy-start.1 = (f32[32,32]{1,0:T(8,128)S(1)}, f32[32,32]{1,0:T(8,128)}, u32[]{:S(2)}) copy-start(f32[32,32]{1,0:T(8,128)} %dense_hbm.1) | copy-start | bytes 12292

commit v3 on v2

--- a/solution.py
+++ b/solution.py
@@ -237,7 +237,7 @@
         compiler_params=pltpu.CompilerParams(
             collective_id=0, has_side_effects=True, vmem_limit_bytes=16 * 2**20
         ),
-    )(row_numbers.T, item_table.T, dense_part, small_ids.reshape(1, EX), small_table)
+    )(*(pltpu.with_memory_space_constraint(a, pltpu.HBM) for a in (row_numbers.T, item_table.T, dense_part, small_ids.reshape(1, EX), small_table)))
     return parts.transpose(1, 0, 2)
 
 

time: 27.8 us -> 25.4 us (0.914)
  local copies, waits for them, and re-layouts: 2.86 us -> 0.61 us
    unnamed x11 -> x1, local copies, waits for them, and re-layouts: 2.86 us -> 0.61 us
where the time goes in v3:
time: 25.4 us; the launch traced here: 25.3 us
  Pallas kernels  24.7 us (97%)
  local copies, waits for them, and re-layouts  0.61 us (2%)
    pallas_call x1, Pallas kernels, shards(): pl.pallas_call(kernel, out_shape=jax.ShapeDtypeStruct((3, EX, F), jnp.bfl...  24.7 us
    unnamed x1, local copies, waits for them, and re-layouts  0.61 us

profile of v3, /device:TPU:2, one launch (start us, length us, event | category | flops | bytes accessed | tf_op | source)
XLA Modules:
  0.0 25.3 jit_solution(8243553884279871595)
XLA Ops:
  0.0 24.7 %shard_map.55 = bf16[3,32,32]{2,1,0:T(8,128)(2,1)S(1)} custom-call(s32[2,32]{1,0:T(2,128)} %bitcast.6, bf16[32,1024]{1,0:T(8,128)(2,1)} %bitcast.5, f32[32,32]{1,0:T(8,128)} %dense_hbm.1, s32[1,32]{1,0:T(1,128)} %bitcast.7, bf16[2,32]{1,0:T(2,128)(2,1)} %small_hbm.1), custom_call_target="tpu_custom_call" | custom-call | tf_op jit(solution)/shard_map/pallas_call | solution.py:215
  24.7 0.6 %copy.7 = bf16[32,3,32]{2,0,1:T(8,128)(2,1)} copy(bf16[32,3,32]{2,0,1:T(8,128)(2,1)S(1)} %bitcast.4) | data formatting | bytes 12288

commit v4 on v3

v4 whole, which is shorter than its diff:
```python
import jax
import jax.numpy as jnp
from jax import lax
from jax.experimental import pallas as pl
from jax.experimental.pallas import tpu as pltpu
from jax.sharding import Mesh
from jax.sharding import PartitionSpec as P

ROW = ("row_0", "row_1", "row_2")
NZ, NY, NX = 8, 4, 4
MESH = pl.DeviceIdType.MESH
BLOCKS = ((0, 0), (1, 0), (0, 1), (0, 3), (1, 1), (1, 3), (0, 2), (1, 2))
FROM = [BLOCKS.index((ky, -kx % NX)) for ky, kx in BLOCKS]
OWNERS = len(BLOCKS)
OFFSETS = sorted(
    ((kz, ky) for kz in range(NZ) for ky in range(2)),
    key=lambda k: (min(k[0], NZ - k[0]) + k[1], k),
)
BACK = [OFFSETS.index((-kz % NZ, ky)) for kz, ky in OFFSETS]
PEERS = len(OFFSETS)
ROWS = 1024
LOW = 256
HIGH = ROWS // LOW
EX = 32
F = 32
CHUNKS = 2
PER = PEERS // CHUNKS
WIDE = PER * 64


def kernel(
    ids_hbm, table_hbm, dense_hbm, sid_hbm, small_hbm, out_ref,
    ids_in, dense, sid, small_in, msg, ids, tab, hot, highs, sums, send, recv, small,
    local_sem, send_sem, tab_sem, ids_sem, row_sem, small_sem, ready,
):
    z, y, x, w = (lax.axis_index(name) for name in (*ROW, "width"))
    odd = lax.rem(y, 2)
    pair_block = z * 2 + y // 2

    def gather_peer(slot, core):
        ky, kx = BLOCKS[slot]
        return (z, y + 1 - 2 * odd if ky else y, lax.rem(x + kx, NX), core)

    def exchange_peer(slot, core):
        kz, ky = OFFSETS[slot]
        return (lax.rem(z + kz, NZ), NY - 1 - y if ky else y, x, core)

    barrier = pltpu.get_barrier_semaphore()
    other = (z, y, x, 1 - w)
    for slot in range(1, OWNERS):
        pl.semaphore_signal(barrier, inc=1, device_id=gather_peer(slot, 0), device_id_type=MESH)
    for slot in range(PEERS - 1, 0, -1):
        pl.semaphore_signal(barrier, inc=1, device_id=exchange_peer(slot, 1), device_id_type=MESH)
    pl.semaphore_signal(barrier, inc=1, device_id=other, device_id_type=MESH)

    fetches = [
        pltpu.make_async_copy(src, dst, local_sem.at[i])
        for i, (src, dst) in enumerate(
            (
                (table_hbm, tab.at[0]), (small_hbm, small_in), (ids_hbm, ids_in),
                (sid_hbm, sid), (dense_hbm, dense),
            )
        )
    ]
    for fetch in fetches:
        fetch.start()

    def push(src, dst, kind, sem, peer):
        pltpu.make_async_remote_copy(
            src_ref=src, dst_ref=dst, send_sem=send_sem.at[kind], recv_sem=sem,
            device_id=peer, device_id_type=MESH,
        ).start()

    def wait(ref, sem):
        pltpu.make_async_copy(ref, ref, sem).wait()

    fetches[1].wait()
    my_two = small.at[pl.ds((pair_block * 8 + odd * NX + x) * 2, 2)]
    my_two[...] = small_in[...].astype(jnp.float32)
    fetches[2].wait()
    pair = ids_in[...]
    line = jnp.concatenate([pair[0:1], pair[1:2], pair[0:1], pair[1:2]], axis=1)
    msg[...] = line
    ids[0:1, :] = line
    fetches[0].wait()
    fetches[3].wait()
    fetches[4].wait()
    out_ref[0] = dense[...].astype(jnp.bfloat16)

    @pl.when(w == 0)
    def _():
        pl.semaphore_wait(barrier, 2 * (OWNERS - 1) + 1)
        pl.semaphore_signal(ready, inc=1, device_id=other, device_id_type=MESH)

    @pl.when(w == 1)
    def _():
        pl.semaphore_wait(ready, 1)

    for slot in range(1, OWNERS):
        push(my_two, my_two, 3, small_sem.at[0], gather_peer(slot, w))
    for slot in range(1, OWNERS):
        push(tab.at[0], tab.at[FROM[slot]], 1, tab_sem.at[FROM[slot] // 4], gather_peer(slot, w))

    @pl.when(w == 1)
    def _():
        pl.semaphore_wait(barrier, 2 * (PEERS - 1) + 1)
        pl.semaphore_signal(ready, inc=1, device_id=other, device_id_type=MESH)

    @pl.when(w == 0)
    def _():
        pl.semaphore_wait(ready, 1)

    for slot in range(PEERS - 1, 0, -1):
        back = BACK[slot]
        push(msg, ids.at[pl.ds(back, 1)], 0, ids_sem.at[back // PER], exchange_peer(slot, w))
    wait(small.at[pl.ds(0, 2 * (OWNERS - 1))], small_sem.at[0])
    my_block = small.at[pl.ds(pl.multiple_of(pair_block * 16, 16), 16)]
    for slot in range(PEERS - 1, 0, -1):
        push(my_block, my_block, 3, small_sem.at[1], exchange_peer(slot, w))

    lane = lax.broadcasted_iota(jnp.int32, (1, 128), 1)
    low_half = lane < 64
    low_half16 = lax.broadcasted_iota(jnp.int32, (16, 128), 1) < 64
    base = pair_block * (OWNERS * ROWS)
    low_rows = lax.broadcasted_iota(jnp.int32, (LOW, WIDE), 0)

    def look_up(chunk, slots, rows):
        lhs = jnp.concatenate(
            [tab[j, :, b * LOW : (b + 1) * LOW] for j in slots for b in range(HIGH)], axis=0
        )
        found = jnp.dot(lhs, hot[chunk], preferred_element_type=jnp.float32)
        high = highs[chunk]
        at = 0
        for j in slots:
            ky, kx = BLOCKS[j]
            owner = (1 - odd if ky else odd) * NX + lax.rem(x + kx, NX)
            for b in range(HIGH):
                rows = jnp.where(high == owner * HIGH + b, found[at : at + F], rows)
                at += F
        return rows

    for chunk in range(CHUNKS):
        first = max(chunk * PER, 1)
        wait(ids.at[pl.ds(first, (chunk + 1) * PER - first)], ids_sem.at[chunk])
        lines = [ids[slot : slot + 1, :] for slot in range(chunk * PER, (chunk + 1) * PER)]
        wanted = jnp.concatenate(
            [jnp.where(low_half, a, b) for a, b in zip(lines[::2], lines[1::2])], axis=1
        ) - base
        highs[chunk] = wanted >> 8
        hot[chunk] = jnp.where(low_rows == (wanted & (LOW - 1)), 1.0, 0.0).astype(jnp.bfloat16)
        if chunk == 0:
            wait(tab.at[pl.ds(1, 3)], tab_sem.at[0])
        sums[chunk] = look_up(chunk, range(4), jnp.zeros((F, WIDE), jnp.float32))

    wait(tab.at[pl.ds(4, 4)], tab_sem.at[1])
    for chunk in range(CHUNKS - 1, -1, -1):
        rows = look_up(chunk, range(4, 8), sums[chunk])
        for half in range(PER // 2):
            part = rows[:, half * 128 : (half + 1) * 128]
            upper, lower = part[:16], part[16:]
            turned_upper = pltpu.roll(upper, 64, 1)
            turned_lower = pltpu.roll(lower, 64, 1)
            slot = chunk * PER + 2 * half
            even = jnp.where(low_half16, upper, turned_lower).astype(jnp.bfloat16)
            if slot:
                send[slot] = even
            else:
                recv[0] = even
            send[slot + 1] = jnp.where(low_half16, turned_upper, lower).astype(jnp.bfloat16)
        for slot in range((chunk + 1) * PER - 1, max(chunk * PER, 1) - 1, -1):
            push(send.at[slot], recv.at[BACK[slot]], 2, row_sem.at[0], exchange_peer(slot, w))

    wait(small.at[pl.ds(0, 16 * (PEERS - 1))], small_sem.at[1])
    small_hot = jnp.where(
        lax.broadcasted_iota(jnp.int32, (256, EX), 0) == sid[...], 1.0, 0.0
    ).astype(jnp.bfloat16)
    out_ref[2] = lax.dot_general(
        small_hot, small[...].astype(jnp.bfloat16), (((0,), (0,)), ((), ())),
        preferred_element_type=jnp.float32,
    ).astype(jnp.bfloat16)

    wait(ids.at[pl.ds(1, PEERS - 1)], send_sem.at[0])
    wait(tab.at[pl.ds(1, OWNERS - 1)], send_sem.at[1])
    wait(small.at[pl.ds(0, 2 * (OWNERS - 1) + 16 * (PEERS - 1))], send_sem.at[3])
    wait(send.at[pl.ds(1, PEERS - 1)], send_sem.at[2])
    wait(recv.at[pl.ds(1, PEERS - 1)], row_sem.at[0])
    total = recv[0].astype(jnp.float32)
    for slot in range(1, PEERS):
        total = total + recv[slot].astype(jnp.float32)
    both = jnp.concatenate(
        [jnp.where(low_half16, total, 0.0), jnp.where(low_half16, 0.0, total)], axis=0
    ).astype(jnp.bfloat16)
    example = lax.broadcasted_iota(jnp.int32, (EX, 128), 0)
    spot = lax.broadcasted_iota(jnp.int32, (EX, 128), 1)
    picks = jnp.where((spot & (EX - 1)) == example, 1.0, 0.0).astype(jnp.bfloat16)
    pooled = lax.dot_general(
        picks, both, (((1,), (1,)), ((), ())), preferred_element_type=jnp.float32
    )
    out_ref[1] = (pooled * 2 ** (-0.5)).astype(jnp.bfloat16)


def shards(row_numbers, item_table, dense_part, small_ids, small_table):
    dma = pltpu.SemaphoreType.DMA
    arrays = row_numbers.T, item_table.T, dense_part, small_ids.reshape(1, EX), small_table
    parts = pl.pallas_call(
        kernel,
        out_shape=jax.ShapeDtypeStruct((3, EX, F), jnp.bfloat16),
        in_specs=[pl.BlockSpec(memory_space=pltpu.HBM)] * 5,
        out_specs=pl.BlockSpec(memory_space=pltpu.VMEM),
        scratch_shapes=[
            pltpu.VMEM((2, EX), jnp.int32),
            pltpu.VMEM((EX, F), jnp.float32),
            pltpu.VMEM((1, EX), jnp.int32),
            pltpu.VMEM((2, F), jnp.bfloat16),
            pltpu.VMEM((1, 128), jnp.int32),
            pltpu.VMEM((PEERS, 128), jnp.int32),
            pltpu.VMEM((OWNERS, F, ROWS), jnp.bfloat16),
            pltpu.VMEM((CHUNKS, LOW, WIDE), jnp.bfloat16),
            pltpu.VMEM((CHUNKS, 1, WIDE), jnp.int32),
            pltpu.VMEM((CHUNKS, F, WIDE), jnp.float32),
            pltpu.VMEM((PEERS, 16, 128), jnp.bfloat16),
            pltpu.VMEM((PEERS, 16, 128), jnp.bfloat16),
            pltpu.VMEM((2 * OWNERS * PEERS, F), jnp.float32),
            dma((5,)), dma((4,)), dma((2,)), dma((CHUNKS,)), dma((1,)), dma((2,)),
            pltpu.SemaphoreType.REGULAR,
        ],
        compiler_params=pltpu.CompilerParams(
            collective_id=0, has_side_effects=True, vmem_limit_bytes=16 * 2**20
        ),
    )(*(pltpu.with_memory_space_constraint(array, pltpu.HBM) for array in arrays))
    return parts.transpose(1, 0, 2)


def solution(mesh):
    torus = Mesh(mesh.devices.reshape(NZ, NY, NX, 2), (*ROW, "width"))
    return jax.shard_map(
        shards,
        mesh=torus,
        in_specs=(P(ROW, None), P(ROW, "width"), P(ROW, "width"), P(ROW), P(ROW, "width")),
        out_specs=P(ROW, None, "width"),
        check_vma=False,
    )
```

time: 25.4 us -> 25.1 us (0.988)
  the two profiles are of different devices: /device:TPU:2 before, /device:TPU:6 now
where the time goes in v4:
time: 25.1 us; the launch traced here: 25 us
  Pallas kernels  24.4 us (97%)
  local copies, waits for them, and re-layouts  0.61 us (2%)
    pallas_call x1, Pallas kernels, shards(): pl.pallas_call(kernel, out_shape=jax.ShapeDtypeStruct((3, EX, F), jnp.bfl...  24.4 us
    unnamed x1, local copies, waits for them, and re-layouts  0.61 us

profile of v4, /device:TPU:6, one launch (start us, length us, event | category | flops | bytes accessed | tf_op | source)
XLA Modules:
  0.0 25.0 jit_solution(11248897983793290495)
XLA Ops:
  0.0 24.4 %shard_map.55 = bf16[3,32,32]{2,1,0:T(8,128)(2,1)S(1)} custom-call(s32[2,32]{1,0:T(2,128)} %bitcast.6, bf16[32,1024]{1,0:T(8,128)(2,1)} %bitcast.5, f32[32,32]{1,0:T(8,128)} %dense_hbm.1, s32[1,32]{1,0:T(1,128)} %bitcast.7, bf16[2,32]{1,0:T(2,128)(2,1)} %small_hbm.1), custom_call_target="tpu_custom_call" | custom-call | tf_op jit(solution)/shard_map/pallas_call | solution.py:205
  24.4 0.6 %copy.7 = bf16[32,3,32]{2,0,1:T(8,128)(2,1)} copy(bf16[32,3,32]{2,0,1:T(8,128)(2,1)S(1)} %bitcast.4) | data formatting | bytes 12288

commit v5 on v4

v5 whole, which is shorter than its diff:
```python
import jax
import jax.numpy as jnp
from jax import lax
from jax.experimental import pallas as pl
from jax.experimental.pallas import tpu as pltpu
from jax.sharding import Mesh
from jax.sharding import PartitionSpec as P

ROW = ("row_0", "row_1", "row_2")
NZ, NY, NX = 8, 4, 4
MESH = pl.DeviceIdType.MESH
OWNERS = NX
OFFSETS = sorted(
    ((kz, ky) for kz in range(NZ) for ky in range(NY)),
    key=lambda k: (min(k[0], NZ - k[0]) + min(k[1], NY - k[1]), k),
)
BACK = [OFFSETS.index((-kz % NZ, -ky % NY)) for kz, ky in OFFSETS]
PEERS = len(OFFSETS)
ROWS = 1024
LOW = 256
HIGH = ROWS // LOW
EX = 32
F = 32
CHUNKS = 4
PER = PEERS // CHUNKS
WIDE = PER * 64


def kernel(
    ids_hbm, table_hbm, dense_hbm, sid_hbm, small_hbm, out_ref,
    ids_in, dense, sid, small_in, msg, ids, tab, send, recv, small,
    local_sem, send_sem, tab_sem, ids_sem, row_sem, small_sem, ready,
):
    z, y, x, w = (lax.axis_index(name) for name in (*ROW, "width"))
    block = z * NY + y

    def gather_peer(slot, core):
        return (z, y, lax.rem(x + slot, NX), core)

    def exchange_peer(slot, core):
        kz, ky = OFFSETS[slot]
        return (lax.rem(z + kz, NZ), lax.rem(y + ky, NY), x, core)

    barrier = pltpu.get_barrier_semaphore()
    other = (z, y, x, 1 - w)
    for slot in range(1, OWNERS):
        pl.semaphore_signal(barrier, inc=1, device_id=gather_peer(slot, 0), device_id_type=MESH)
    for slot in range(PEERS - 1, 0, -1):
        pl.semaphore_signal(barrier, inc=1, device_id=exchange_peer(slot, 1), device_id_type=MESH)
    pl.semaphore_signal(barrier, inc=1, device_id=other, device_id_type=MESH)

    fetches = [
        pltpu.make_async_copy(src, dst, local_sem.at[i])
        for i, (src, dst) in enumerate(
            (
                (table_hbm, tab.at[0]), (small_hbm, small_in), (ids_hbm, ids_in),
                (sid_hbm, sid), (dense_hbm, dense),
            )
        )
    ]
    for fetch in fetches:
        fetch.start()

    def push(src, dst, kind, sem, peer):
        pltpu.make_async_remote_copy(
            src_ref=src, dst_ref=dst, send_sem=send_sem.at[kind], recv_sem=sem,
            device_id=peer, device_id_type=MESH,
        ).start()

    def wait(ref, sem):
        pltpu.make_async_copy(ref, ref, sem).wait()

    fetches[1].wait()
    two = small_in[...].astype(jnp.float32)
    my_line = small.at[pl.ds(block * NX + x, 1)]
    my_line[...] = jnp.concatenate([two[0:1], two[1:2], two[0:1], two[1:2]], axis=1)
    fetches[2].wait()
    pair = ids_in[...]
    line = jnp.concatenate([pair[0:1], pair[1:2], pair[0:1], pair[1:2]], axis=1)
    msg[...] = line
    ids[0:1, :] = line
    fetches[0].wait()
    fetches[3].wait()
    fetches[4].wait()
    out_ref[0] = dense[...].astype(jnp.bfloat16)

    @pl.when(w == 0)
    def _():
        pl.semaphore_wait(barrier, 2 * (OWNERS - 1) + 1)
        pl.semaphore_signal(ready, inc=1, device_id=other, device_id_type=MESH)

    @pl.when(w == 1)
    def _():
        pl.semaphore_wait(ready, 1)

    for slot in range(1, OWNERS):
        push(my_line, my_line, 3, small_sem.at[0], gather_peer(slot, w))
    for slot in range(OWNERS - 1, 0, -1):
        push(tab.at[0], tab.at[NX - slot], 1, tab_sem.at[0], gather_peer(slot, w))

    @pl.when(w == 1)
    def _():
        pl.semaphore_wait(barrier, 2 * (PEERS - 1) + 1)
        for slot in range(PEERS - 1, 0, -1):
            back = BACK[slot]
            for core in (1, 0):
                push(
                    msg, ids.at[pl.ds(back, 1)], 0, ids_sem.at[back // PER],
                    exchange_peer(slot, core),
                )
        pl.semaphore_signal(ready, inc=1, device_id=other, device_id_type=MESH)

    @pl.when(w == 0)
    def _():
        pl.semaphore_wait(ready, 1)

    wait(small.at[pl.ds(0, OWNERS - 1)], small_sem.at[0])
    my_block = small.at[pl.ds(block * OWNERS, OWNERS)]
    for slot in range(PEERS - 1, 0, -1):
        push(my_block, my_block, 3, small_sem.at[1], exchange_peer(slot, w))

    lane = lax.broadcasted_iota(jnp.int32, (1, 128), 1)
    low_half = lane < 64
    low_half16 = lax.broadcasted_iota(jnp.int32, (16, 128), 1) < 64
    low_rows = lax.broadcasted_iota(jnp.int32, (LOW, WIDE), 0)

    for chunk in range(CHUNKS):
        first = max(chunk * PER, 1)
        slots = range((chunk + 1) * PER - 1, first - 1, -1)
        wait(ids.at[pl.ds(first, len(slots))], ids_sem.at[chunk])
        lines = [ids[slot : slot + 1, :] for slot in range(chunk * PER, (chunk + 1) * PER)]
        wanted = jnp.concatenate(
            [jnp.where(low_half, a, b) for a, b in zip(lines[::2], lines[1::2])], axis=1
        )
        high = wanted >> 8
        hot = jnp.where(low_rows == (wanted & (LOW - 1)), 1.0, 0.0).astype(jnp.bfloat16)
        if chunk == 0:
            wait(tab.at[pl.ds(1, OWNERS - 1)], tab_sem.at[0])
        lhs = jnp.concatenate(
            [tab[j, :, b * LOW : (b + 1) * LOW] for j in range(OWNERS) for b in range(HIGH)], axis=0
        )
        found = jnp.dot(lhs, hot, preferred_element_type=jnp.float32)
        rows = jnp.zeros((F, WIDE), jnp.float32)
        for j in range(OWNERS):
            owner = block * NX + lax.rem(x + j, NX)
            for b in range(HIGH):
                at = (j * HIGH + b) * F
                here = owner * HIGH + b
                rows = jnp.where(high == here, found[at : at + F], rows)
        for half in range(PER // 2):
            part = rows[:, half * 128 : (half + 1) * 128]
            upper, lower = part[:16], part[16:]
            turned_upper = pltpu.roll(upper, 64, 1)
            turned_lower = pltpu.roll(lower, 64, 1)
            slot = chunk * PER + 2 * half
            even = jnp.where(low_half16, upper, turned_lower).astype(jnp.bfloat16)
            if slot:
                send[slot] = even
            else:
                recv[0] = even
            send[slot + 1] = jnp.where(low_half16, turned_upper, lower).astype(jnp.bfloat16)
        for slot in slots:
            push(send.at[slot], recv.at[BACK[slot]], 2, row_sem.at[0], exchange_peer(slot, w))

    wait(small.at[pl.ds(0, OWNERS * (PEERS - 1))], small_sem.at[1])
    wanted = sid[...]
    lines = small[...].astype(jnp.bfloat16)
    small_rows = jnp.zeros((EX, F), jnp.float32)
    for row in range(2):
        spot = jnp.where((wanted & 1) == row, wanted >> 1, -1)
        small_hot = jnp.where(
            lax.broadcasted_iota(jnp.int32, (OWNERS * PEERS, EX), 0) == spot, 1.0, 0.0
        ).astype(jnp.bfloat16)
        small_rows = small_rows + lax.dot_general(
            small_hot, lines[:, row * F : (row + 1) * F], (((0,), (0,)), ((), ())),
            preferred_element_type=jnp.float32,
        )
    out_ref[2] = small_rows.astype(jnp.bfloat16)

    @pl.when(w == 1)
    def _():
        for _ in range(2):
            wait(ids.at[pl.ds(1, PEERS - 1)], send_sem.at[0])

    wait(tab.at[pl.ds(1, OWNERS - 1)], send_sem.at[1])
    wait(small.at[pl.ds(0, OWNERS * PEERS - 1)], send_sem.at[3])
    wait(send.at[pl.ds(1, PEERS - 1)], send_sem.at[2])
    wait(recv.at[pl.ds(1, PEERS - 1)], row_sem.at[0])
    total = recv[0].astype(jnp.float32)
    for slot in range(1, PEERS):
        total = total + recv[slot].astype(jnp.float32)
    both = jnp.concatenate(
        [jnp.where(low_half16, total, 0.0), jnp.where(low_half16, 0.0, total)], axis=0
    ).astype(jnp.bfloat16)
    example = lax.broadcasted_iota(jnp.int32, (EX, 128), 0)
    spot = lax.broadcasted_iota(jnp.int32, (EX, 128), 1)
    picks = jnp.where((spot & (EX - 1)) == example, 1.0, 0.0).astype(jnp.bfloat16)
    pooled = lax.dot_general(
        picks, both, (((1,), (1,)), ((), ())), preferred_element_type=jnp.float32
    )
    out_ref[1] = (pooled * 2 ** (-0.5)).astype(jnp.bfloat16)


def shards(row_numbers, item_table, dense_part, small_ids, small_table):
    dma = pltpu.SemaphoreType.DMA
    arrays = row_numbers.T, item_table.T, dense_part, small_ids.reshape(1, EX), small_table
    parts = pl.pallas_call(
        kernel,
        out_shape=jax.ShapeDtypeStruct((3, EX, F), jnp.bfloat16),
        in_specs=[pl.BlockSpec(memory_space=pltpu.HBM)] * 5,
        out_specs=pl.BlockSpec(memory_space=pltpu.VMEM),
        scratch_shapes=[
            pltpu.VMEM((2, EX), jnp.int32),
            pltpu.VMEM((EX, F), jnp.float32),
            pltpu.VMEM((1, EX), jnp.int32),
            pltpu.VMEM((2, F), jnp.bfloat16),
            pltpu.VMEM((1, 128), jnp.int32),
            pltpu.VMEM((PEERS, 128), jnp.int32),
            pltpu.VMEM((OWNERS, F, ROWS), jnp.bfloat16),
            pltpu.VMEM((PEERS, 16, 128), jnp.bfloat16),
            pltpu.VMEM((PEERS, 16, 128), jnp.bfloat16),
            pltpu.VMEM((OWNERS * PEERS, 128), jnp.float32),
            dma((5,)), dma((4,)), dma((1,)), dma((CHUNKS,)), dma((1,)), dma((2,)),
            pltpu.SemaphoreType.REGULAR,
        ],
        compiler_params=pltpu.CompilerParams(
            collective_id=0, has_side_effects=True, vmem_limit_bytes=16 * 2**20
        ),
    )(*(pltpu.with_memory_space_constraint(array, pltpu.HBM) for array in arrays))
    return parts.transpose(1, 0, 2)


def solution(mesh):
    torus = Mesh(mesh.devices.reshape(NZ, NY, NX, 2), (*ROW, "width"))
    return jax.shard_map(
        shards,
        mesh=torus,
        in_specs=(P(ROW, None), P(ROW, "width"), P(ROW, "width"), P(ROW), P(ROW, "width")),
        out_specs=P(ROW, None, "width"),
        check_vma=False,
    )
```

time: 25.1 us -> 23 us (0.916)
  the two profiles are of different devices: /device:TPU:6 before, /device:TPU:1 now
where the time goes in v5:
time: 23 us; the launch traced here: 22.9 us
  Pallas kernels  22.3 us (97%)
  local copies, waits for them, and re-layouts  0.61 us (3%)
    pallas_call x1, Pallas kernels, shards(): pl.pallas_call(kernel, out_shape=jax.ShapeDtypeStruct((3, EX, F), jnp.bfl...  22.3 us
    unnamed x1, local copies, waits for them, and re-layouts  0.61 us

profile of v5, /device:TPU:1, one launch (start us, length us, event | category | flops | bytes accessed | tf_op | source)
XLA Modules:
  0.0 22.9 jit_solution(664687857601306542)
XLA Ops:
  0.0 22.3 %shard_map.55 = bf16[3,32,32]{2,1,0:T(8,128)(2,1)S(1)} custom-call(s32[2,32]{1,0:T(2,128)} %bitcast.6, bf16[32,1024]{1,0:T(8,128)(2,1)} %bitcast.5, f32[32,32]{1,0:T(8,128)} %dense_hbm.1, s32[1,32]{1,0:T(1,128)} %bitcast.7, bf16[2,32]{1,0:T(2,128)(2,1)} %small_hbm.1), custom_call_target="tpu_custom_call" | custom-call | tf_op jit(solution)/shard_map/pallas_call | solution.py:207
  22.3 0.6 %copy.7 = bf16[32,3,32]{2,0,1:T(8,128)(2,1)} copy(bf16[32,3,32]{2,0,1:T(8,128)(2,1)S(1)} %bitcast.4) | data formatting | bytes 12288

commit v6 on v5

--- a/solution.py
+++ b/solution.py
@@ -10,19 +10,17 @@
 NZ, NY, NX = 8, 4, 4
 MESH = pl.DeviceIdType.MESH
 OWNERS = NX
-OFFSETS = sorted(
-    ((kz, ky) for kz in range(NZ) for ky in range(NY)),
-    key=lambda k: (min(k[0], NZ - k[0]) + min(k[1], NY - k[1]), k),
-)
-BACK = [OFFSETS.index((-kz % NZ, -ky % NY)) for kz, ky in OFFSETS]
-PEERS = len(OFFSETS)
+PEERS = NZ * NY
+FAR_Z = (4, 3, 5, 2, 6, 1, 7, 0)
+FAR_Y = (2, 1, 3, 0)
 ROWS = 1024
 LOW = 256
 HIGH = ROWS // LOW
 EX = 32
 F = 32
-CHUNKS = 4
-PER = PEERS // CHUNKS
+CHUNKS = 8
+PLANES = NZ // CHUNKS
+PER = PLANES * NY
 WIDE = PER * 64
 
 
@@ -37,16 +35,20 @@
     def gather_peer(slot, core):
         return (z, y, lax.rem(x + slot, NX), core)
 
-    def exchange_peer(slot, core):
-        kz, ky = OFFSETS[slot]
-        return (lax.rem(z + kz, NZ), lax.rem(y + ky, NY), x, core)
+    def exchange_peer(plane, ky, core):
+        return (plane, lax.rem(y + ky, NY), x, core)
+
+    def my_slot(ky):
+        return z * NY + -ky % NY
 
     barrier = pltpu.get_barrier_semaphore()
     other = (z, y, x, 1 - w)
     for slot in range(1, OWNERS):
         pl.semaphore_signal(barrier, inc=1, device_id=gather_peer(slot, 0), device_id_type=MESH)
-    for slot in range(PEERS - 1, 0, -1):
-        pl.semaphore_signal(barrier, inc=1, device_id=exchange_peer(slot, 1), device_id_type=MESH)
+    others = [(kz, ky) for kz in FAR_Z for ky in FAR_Y if kz or ky]
+    for kz, ky in others:
+        peer = exchange_peer(lax.rem(z + kz, NZ), ky, 1)
+        pl.semaphore_signal(barrier, inc=1, device_id=peer, device_id_type=MESH)
     pl.semaphore_signal(barrier, inc=1, device_id=other, device_id_type=MESH)
 
     fetches = [
@@ -78,7 +80,7 @@
     pair = ids_in[...]
     line = jnp.concatenate([pair[0:1], pair[1:2], pair[0:1], pair[1:2]], axis=1)
     msg[...] = line
-    ids[0:1, :] = line
+    pltpu.make_async_copy(msg, ids.at[pl.ds(my_slot(0), 1)], ids_sem.at[z // PLANES]).start()
     fetches[0].wait()
     fetches[3].wait()
     fetches[4].wait()
@@ -101,12 +103,11 @@
     @pl.when(w == 1)
     def _():
         pl.semaphore_wait(barrier, 2 * (PEERS - 1) + 1)
-        for slot in range(PEERS - 1, 0, -1):
-            back = BACK[slot]
+        for kz, ky in others:
             for core in (1, 0):
                 push(
-                    msg, ids.at[pl.ds(back, 1)], 0, ids_sem.at[back // PER],
-                    exchange_peer(slot, core),
+                    msg, ids.at[pl.ds(my_slot(ky), 1)], 0, ids_sem.at[z // PLANES],
+                    exchange_peer(lax.rem(z + kz, NZ), ky, core),
                 )
         pl.semaphore_signal(ready, inc=1, device_id=other, device_id_type=MESH)
 
@@ -116,8 +117,8 @@
 
     wait(small.at[pl.ds(0, OWNERS - 1)], small_sem.at[0])
     my_block = small.at[pl.ds(block * OWNERS, OWNERS)]
-    for slot in range(PEERS - 1, 0, -1):
-        push(my_block, my_block, 3, small_sem.at[1], exchange_peer(slot, w))
+    for kz, ky in others:
+        push(my_block, my_block, 3, small_sem.at[1], exchange_peer(lax.rem(z + kz, NZ), ky, w))
 
     lane = lax.broadcasted_iota(jnp.int32, (1, 128), 1)
     low_half = lane < 64
@@ -125,9 +126,7 @@
     low_rows = lax.broadcasted_iota(jnp.int32, (LOW, WIDE), 0)
 
     for chunk in range(CHUNKS):
-        first = max(chunk * PER, 1)
-        slots = range((chunk + 1) * PER - 1, first - 1, -1)
-        wait(ids.at[pl.ds(first, len(slots))], ids_sem.at[chunk])
+        wait(ids.at[pl.ds(chunk * PER, PER)], ids_sem.at[chunk])
         lines = [ids[slot : slot + 1, :] for slot in range(chunk * PER, (chunk + 1) * PER)]
         wanted = jnp.concatenate(
             [jnp.where(low_half, a, b) for a, b in zip(lines[::2], lines[1::2])], axis=1
@@ -153,14 +152,22 @@
             turned_upper = pltpu.roll(upper, 64, 1)
             turned_lower = pltpu.roll(lower, 64, 1)
             slot = chunk * PER + 2 * half
-            even = jnp.where(low_half16, upper, turned_lower).astype(jnp.bfloat16)
-            if slot:
-                send[slot] = even
-            else:
-                recv[0] = even
+            send[slot] = jnp.where(low_half16, upper, turned_lower).astype(jnp.bfloat16)
             send[slot + 1] = jnp.where(low_half16, turned_upper, lower).astype(jnp.bfloat16)
-        for slot in slots:
-            push(send.at[slot], recv.at[BACK[slot]], 2, row_sem.at[0], exchange_peer(slot, w))
+        for plane in range(chunk * PLANES, (chunk + 1) * PLANES):
+            for ky in FAR_Y:
+                source, target = send.at[plane * NY + ky], recv.at[my_slot(ky)]
+                if ky:
+                    push(source, target, 2, row_sem.at[0], exchange_peer(plane, ky, w))
+                    continue
+
+                @pl.when(plane != z)
+                def _():
+                    push(source, target, 2, row_sem.at[0], exchange_peer(plane, ky, w))
+
+                @pl.when(plane == z)
+                def _():
+                    pltpu.make_async_copy(source, target, row_sem.at[0]).start()
 
     wait(small.at[pl.ds(0, OWNERS * (PEERS - 1))], small_sem.at[1])
     wanted = sid[...]
@@ -185,7 +192,7 @@
     wait(tab.at[pl.ds(1, OWNERS - 1)], send_sem.at[1])
     wait(small.at[pl.ds(0, OWNERS * PEERS - 1)], send_sem.at[3])
     wait(send.at[pl.ds(1, PEERS - 1)], send_sem.at[2])
-    wait(recv.at[pl.ds(1, PEERS - 1)], row_sem.at[0])
+    wait(recv.at[pl.ds(0, PEERS)], row_sem.at[0])
     total = recv[0].astype(jnp.float32)
     for slot in range(1, PEERS):
         total = total + recv[slot].astype(jnp.float32)

time: 23 us -> 22.3 us (0.970)
  Pallas kernels: 22.3 us -> 21.4 us
    pallas_call x1, Pallas kernels: 22.3 us -> 21.4 us  [shards(): pl.pallas_call(kernel, out_shape=jax.ShapeDtypeStruct((3, EX, F), jnp.bfl...]
where the time goes in v6:
time: 22.3 us; the launch traced here: 22 us
  Pallas kernels  21.4 us (96%)
  local copies, waits for them, and re-layouts  0.61 us (3%)
    pallas_call x1, Pallas kernels, shards(): pl.pallas_call(kernel, out_shape=jax.ShapeDtypeStruct((3, EX, F), jnp.bfl...  21.4 us
    unnamed x1, local copies, waits for them, and re-layouts  0.61 us

profile of v6, /device:TPU:1, one launch (start us, length us, event | category | flops | bytes accessed | tf_op | source)
XLA Modules:
  0.0 22.0 jit_solution(7166575972529563707)
XLA Ops:
  0.0 21.4 %shard_map.55 = bf16[3,32,32]{2,1,0:T(8,128)(2,1)S(1)} custom-call(s32[2,32]{1,0:T(2,128)} %bitcast.6, bf16[32,1024]{1,0:T(8,128)(2,1)} %bitcast.5, f32[32,32]{1,0:T(8,128)} %dense_hbm.1, s32[1,32]{1,0:T(1,128)} %bitcast.7, bf16[2,32]{1,0:T(2,128)(2,1)} %small_hbm.1), custom_call_target="tpu_custom_call" | custom-call | tf_op jit(solution)/shard_map/pallas_call | solution.py:214
  21.4 0.6 %copy.7 = bf16[32,3,32]{2,0,1:T(8,128)(2,1)} copy(bf16[32,3,32]{2,0,1:T(8,128)(2,1)S(1)} %bitcast.4) | data formatting | bytes 12288

commit v7 on v6

v7 whole, which is shorter than its diff:
```python
import jax
import jax.numpy as jnp
from jax import lax
from jax.experimental import pallas as pl
from jax.experimental.pallas import tpu as pltpu
from jax.sharding import Mesh
from jax.sharding import PartitionSpec as P

ROW = ("row_0", "row_1", "row_2")
NZ, NY, NX = 8, 4, 4
MESH = pl.DeviceIdType.MESH
BLOCKS = ((0, 0), (0, 1), (1, 0), (1, 1))
OWNERS = len(BLOCKS)
SIDES = len(BLOCKS)
PEERS = NZ * SIDES
FAR_Z = (4, 3, 5, 2, 6, 1, 7)
FAR_SIDE = (3, 1, 2, 0)
ROWS = 1024
LOW = 256
HIGH = ROWS // LOW
EX = 32
F = 32
WIDE = SIDES * 64


def kernel(
    ids_hbm, table_hbm, dense_hbm, sid_hbm, small_hbm, out_ref,
    ids_in, dense, sid, small_in, ring, ids, tab, send, recv, small,
    local_sem, send_sem, tab_sem, ring_sem, ids_sem, row_sem, small_sem, ready,
):
    z, y, x, w = (lax.axis_index(name) for name in (*ROW, "width"))
    odd_y, odd_x = lax.rem(y, 2), lax.rem(x, 2)
    half_y, half_x = y // 2, x // 2
    quarter = half_y * 2 + half_x
    block = z * SIDES + quarter

    def owner(slot):
        fy, fx = BLOCKS[slot]
        return y + 1 - 2 * odd_y if fy else y, x + 1 - 2 * odd_x if fx else x

    def gather_peer(slot, core):
        return (z, *owner(slot), core)

    def mirror_peer(plane, side, core):
        my, mx = BLOCKS[side]
        return (plane, NY - 1 - y if my else y, NX - 1 - x if mx else x, core)

    def mirror_line(side):
        my, mx = BLOCKS[side]
        return (1 - half_y if my else half_y) * 2 + (1 - half_x if mx else half_x)

    def z_peer(kz, core):
        return (lax.rem(z + kz, NZ), y, x, core)

    barrier = pltpu.get_barrier_semaphore()
    other = (z, y, x, 1 - w)
    for kz in FAR_Z:
        pl.semaphore_signal(barrier, inc=1, device_id=z_peer(kz, 1), device_id_type=MESH)
    for slot in range(1, OWNERS):
        pl.semaphore_signal(barrier, inc=1, device_id=gather_peer(slot, 0), device_id_type=MESH)
    pl.semaphore_signal(barrier, inc=1, device_id=other, device_id_type=MESH)

    @pl.when(w == 1)
    def _():
        for side in range(1, SIDES):
            peer = mirror_peer(z, side, 0)
            pl.semaphore_signal(barrier, inc=1, device_id=peer, device_id_type=MESH)


    fetches = [
        pltpu.make_async_copy(src, dst, local_sem.at[i])
        for i, (src, dst) in enumerate(
            (
                (table_hbm, tab.at[0]), (small_hbm, small_in), (ids_hbm, ids_in),
                (sid_hbm, sid), (dense_hbm, dense),
            )
        )
    ]
    for fetch in fetches:
        fetch.start()

    def push(src, dst, kind, sem, peer):
        pltpu.make_async_remote_copy(
            src_ref=src, dst_ref=dst, send_sem=send_sem.at[kind], recv_sem=sem,
            device_id=peer, device_id_type=MESH,
        ).start()

    def wait(ref, sem):
        pltpu.make_async_copy(ref, ref, sem).wait()

    fetches[1].wait()
    two = small_in[...].astype(jnp.float32)
    my_line = small.at[pl.ds(block * OWNERS + odd_y * 2 + odd_x, 1)]
    my_line[...] = jnp.concatenate([two[0:1], two[1:2], two[0:1], two[1:2]], axis=1)
    fetches[2].wait()
    pair = ids_in[...]
    line = jnp.concatenate([pair[0:1], pair[1:2], pair[0:1], pair[1:2]], axis=1)
    my_ring = ring.at[pl.ds(quarter, 1)]
    my_ring[...] = line
    fetches[0].wait()
    fetches[3].wait()
    fetches[4].wait()
    out_ref[0] = dense[...].astype(jnp.bfloat16)

    @pl.when(w == 0)
    def _():
        pl.semaphore_wait(barrier, 2 * (OWNERS - 1) + SIDES)
        pl.semaphore_signal(ready, inc=1, device_id=other, device_id_type=MESH)

    @pl.when(w == 1)
    def _():
        pl.semaphore_wait(ready, 1)
        for side in FAR_SIDE[:-1]:
            push(my_ring, my_ring, 0, ring_sem.at[0], mirror_peer(z, side, 1))

    for slot in range(1, OWNERS):
        push(my_line, my_line, 3, small_sem.at[0], gather_peer(slot, w))
    for slot in range(OWNERS - 1, 0, -1):
        push(tab.at[0], tab.at[slot], 1, tab_sem.at[0], gather_peer(slot, w))

    @pl.when(w == 1)
    def _():
        bundle = ids.at[pl.ds(z * SIDES, SIDES)]
        pl.semaphore_wait(barrier, 2 * (NZ - 1) + 1)
        wait(ring.at[pl.ds(0, SIDES - 1)], ring_sem.at[0])
        for kz in FAR_Z:
            for core in (1, 0):
                push(ring, bundle, 0, ids_sem.at[z], z_peer(kz, core))
        push(ring, bundle, 0, ids_sem.at[z], other)
        pltpu.make_async_copy(ring, bundle, ids_sem.at[z]).start()

    wait(small.at[pl.ds(0, OWNERS - 1)], small_sem.at[0])
    my_block = small.at[pl.ds(block * OWNERS, OWNERS)]

    lane = lax.broadcasted_iota(jnp.int32, (1, 128), 1)
    low_half = lane < 64
    low_half16 = lax.broadcasted_iota(jnp.int32, (16, 128), 1) < 64
    low_rows = lax.broadcasted_iota(jnp.int32, (LOW, WIDE), 0)

    for plane in range(NZ):
        wait(ids.at[pl.ds(plane * SIDES, SIDES)], ids_sem.at[plane])
        for side in FAR_SIDE:
            if side:
                push(my_block, my_block, 3, small_sem.at[1], mirror_peer(plane, side, w))
                continue

            @pl.when(plane != z)
            def _():
                push(my_block, my_block, 3, small_sem.at[1], mirror_peer(plane, side, w))

        lines = [ids[pl.ds(plane * SIDES + mirror_line(side), 1), :] for side in range(SIDES)]
        wanted = jnp.concatenate(
            [jnp.where(low_half, a, b) for a, b in zip(lines[::2], lines[1::2])], axis=1
        )
        high = wanted >> 8
        hot = jnp.where(low_rows == (wanted & (LOW - 1)), 1.0, 0.0).astype(jnp.bfloat16)
        if plane == 0:
            wait(tab.at[pl.ds(1, OWNERS - 1)], tab_sem.at[0])
        lhs = jnp.concatenate(
            [tab[j, :, b * LOW : (b + 1) * LOW] for j in range(OWNERS) for b in range(HIGH)], axis=0
        )
        found = jnp.dot(lhs, hot, preferred_element_type=jnp.float32)
        rows = jnp.zeros((F, WIDE), jnp.float32)
        for j in range(OWNERS):
            yo, xo = owner(j)
            for b in range(HIGH):
                at = (j * HIGH + b) * F
                here = ((z * NY + yo) * NX + xo) * HIGH + b
                rows = jnp.where(high == here, found[at : at + F], rows)
        for half in range(SIDES // 2):
            part = rows[:, half * 128 : (half + 1) * 128]
            upper, lower = part[:16], part[16:]
            turned_upper = pltpu.roll(upper, 64, 1)
            turned_lower = pltpu.roll(lower, 64, 1)
            slot = plane * SIDES + 2 * half
            send[slot] = jnp.where(low_half16, upper, turned_lower).astype(jnp.bfloat16)
            send[slot + 1] = jnp.where(low_half16, turned_upper, lower).astype(jnp.bfloat16)
        for side in FAR_SIDE:
            source, target = send.at[plane * SIDES + side], recv.at[block]
            if side:
                push(source, target, 2, row_sem.at[0], mirror_peer(plane, side, w))
                continue

            @pl.when(plane != z)
            def _():
                push(source, target, 2, row_sem.at[0], mirror_peer(plane, side, w))

            @pl.when(plane == z)
            def _():
                pltpu.make_async_copy(source, target, row_sem.at[0]).start()

    wait(small.at[pl.ds(0, OWNERS * (PEERS - 1))], small_sem.at[1])
    wanted = sid[...]
    device = wanted >> 1
    line = (device & 0x79) | ((device & 2) << 1) | ((device & 4) >> 1)
    lines = small[...].astype(jnp.bfloat16)
    small_rows = jnp.zeros((EX, F), jnp.float32)
    for row in range(2):
        spot = jnp.where((wanted & 1) == row, line, -1)
        small_hot = jnp.where(
            lax.broadcasted_iota(jnp.int32, (OWNERS * PEERS, EX), 0) == spot, 1.0, 0.0
        ).astype(jnp.bfloat16)
        small_rows = small_rows + lax.dot_general(
            small_hot, lines[:, row * F : (row + 1) * F], (((0,), (0,)), ((), ())),
            preferred_element_type=jnp.float32,
        )
    out_ref[2] = small_rows.astype(jnp.bfloat16)

    @pl.when(w == 1)
    def _():
        wait(ids.at[pl.ds(0, PEERS)], send_sem.at[0])
        wait(ids.at[pl.ds(0, PEERS - 1)], send_sem.at[0])

    wait(tab.at[pl.ds(1, OWNERS - 1)], send_sem.at[1])
    wait(small.at[pl.ds(0, OWNERS * PEERS - 1)], send_sem.at[3])
    wait(send.at[pl.ds(1, PEERS - 1)], send_sem.at[2])
    wait(recv.at[pl.ds(0, PEERS)], row_sem.at[0])
    total = recv[0].astype(jnp.float32)
    for slot in range(1, PEERS):
        total = total + recv[slot].astype(jnp.float32)
    both = jnp.concatenate(
        [jnp.where(low_half16, total, 0.0), jnp.where(low_half16, 0.0, total)], axis=0
    ).astype(jnp.bfloat16)
    example = lax.broadcasted_iota(jnp.int32, (EX, 128), 0)
    spot = lax.broadcasted_iota(jnp.int32, (EX, 128), 1)
    picks = jnp.where((spot & (EX - 1)) == example, 1.0, 0.0).astype(jnp.bfloat16)
    pooled = lax.dot_general(
        picks, both, (((1,), (1,)), ((), ())), preferred_element_type=jnp.float32
    )
    out_ref[1] = (pooled * 2 ** (-0.5)).astype(jnp.bfloat16)


def shards(row_numbers, item_table, dense_part, small_ids, small_table):
    dma = pltpu.SemaphoreType.DMA
    arrays = row_numbers.T, item_table.T, dense_part, small_ids.reshape(1, EX), small_table
    parts = pl.pallas_call(
        kernel,
        out_shape=jax.ShapeDtypeStruct((3, EX, F), jnp.bfloat16),
        in_specs=[pl.BlockSpec(memory_space=pltpu.HBM)] * 5,
        out_specs=pl.BlockSpec(memory_space=pltpu.VMEM),
        scratch_shapes=[
            pltpu.VMEM((2, EX), jnp.int32),
            pltpu.VMEM((EX, F), jnp.float32),
            pltpu.VMEM((1, EX), jnp.int32),
            pltpu.VMEM((2, F), jnp.bfloat16),
            pltpu.VMEM((SIDES, 128), jnp.int32),
            pltpu.VMEM((PEERS, 128), jnp.int32),
            pltpu.VMEM((OWNERS, F, ROWS), jnp.bfloat16),
            pltpu.VMEM((PEERS, 16, 128), jnp.bfloat16),
            pltpu.VMEM((PEERS, 16, 128), jnp.bfloat16),
            pltpu.VMEM((OWNERS * PEERS, 128), jnp.float32),
            dma((5,)), dma((4,)), dma((1,)), dma((1,)), dma((NZ,)), dma((1,)), dma((2,)),
            pltpu.SemaphoreType.REGULAR,
        ],
        compiler_params=pltpu.CompilerParams(
            collective_id=0, has_side_effects=True, vmem_limit_bytes=16 * 2**20
        ),
    )(*(pltpu.with_memory_space_constraint(array, pltpu.HBM) for array in arrays))
    return parts.transpose(1, 0, 2)


def solution(mesh):
    torus = Mesh(mesh.devices.reshape(NZ, NY, NX, 2), (*ROW, "width"))
    return jax.shard_map(
        shards,
        mesh=torus,
        in_specs=(P(ROW, None), P(ROW, "width"), P(ROW, "width"), P(ROW), P(ROW, "width")),
        out_specs=P(ROW, None, "width"),
        check_vma=False,
    )
```

time: 22.3 us -> 22.8 us (1.022)
  the two profiles are of different devices: /device:TPU:1 before, /device:TPU:225 now
where the time goes in v7:
time: 22.8 us; the launch traced here: 22.7 us
  Pallas kernels  22 us (96%)
  local copies, waits for them, and re-layouts  0.61 us (3%)
    pallas_call x1, Pallas kernels, shards(): pl.pallas_call(kernel, out_shape=jax.ShapeDtypeStruct((3, EX, F), jnp.bfl...  22 us
    unnamed x1, local copies, waits for them, and re-layouts  0.61 us

profile of v7, /device:TPU:225, one launch (start us, length us, event | category | flops | bytes accessed | tf_op | source)
XLA Modules:
  0.0 22.7 jit_solution(14870665427399608302)
XLA Ops:
  0.0 22.0 %shard_map.55 = bf16[3,32,32]{2,1,0:T(8,128)(2,1)S(1)} custom-call(s32[2,32]{1,0:T(2,128)} %bitcast.6, bf16[32,1024]{1,0:T(8,128)(2,1)} %bitcast.5, f32[32,32]{1,0:T(8,128)} %dense_hbm.1, s32[1,32]{1,0:T(1,128)} %bitcast.7, bf16[2,32]{1,0:T(2,128)(2,1)} %small_hbm.1), custom_call_target="tpu_custom_call" | custom-call | tf_op jit(solution)/shard_map/pallas_call | solution.py:236
  22.0 0.6 %copy.7 = bf16[32,3,32]{2,0,1:T(8,128)(2,1)} copy(bf16[32,3,32]{2,0,1:T(8,128)(2,1)S(1)} %bitcast.4) | data formatting | bytes 12288

commit v8 on v7

--- a/solution.py
+++ b/solution.py
@@ -29,23 +29,28 @@
     local_sem, send_sem, tab_sem, ring_sem, ids_sem, row_sem, small_sem, ready,
 ):
     z, y, x, w = (lax.axis_index(name) for name in (*ROW, "width"))
-    odd_y, odd_x = lax.rem(y, 2), lax.rem(x, 2)
-    half_y, half_x = y // 2, x // 2
+    far_y, far_x = y // 2, x // 2
+    half_y, half_x = y + far_y * (3 - 2 * y), x + far_x * (3 - 2 * x)
     quarter = half_y * 2 + half_x
     block = z * SIDES + quarter
 
     def owner(slot):
         fy, fx = BLOCKS[slot]
-        return y + 1 - 2 * odd_y if fy else y, x + 1 - 2 * odd_x if fx else x
+        return NY - 1 - y if fy else y, NX - 1 - x if fx else x
 
     def gather_peer(slot, core):
         return (z, *owner(slot), core)
 
-    def mirror_peer(plane, side, core):
+    def near_peer(plane, side, core):
         my, mx = BLOCKS[side]
-        return (plane, NY - 1 - y if my else y, NX - 1 - x if mx else x, core)
-
-    def mirror_line(side):
+        return (
+            plane,
+            y + 1 - 2 * lax.rem(y, 2) if my else y,
+            x + 1 - 2 * lax.rem(x, 2) if mx else x,
+            core,
+        )
+
+    def near_line(side):
         my, mx = BLOCKS[side]
         return (1 - half_y if my else half_y) * 2 + (1 - half_x if mx else half_x)
 
@@ -63,7 +68,7 @@
     @pl.when(w == 1)
     def _():
         for side in range(1, SIDES):
-            peer = mirror_peer(z, side, 0)
+            peer = near_peer(z, side, 0)
             pl.semaphore_signal(barrier, inc=1, device_id=peer, device_id_type=MESH)
 
 
@@ -90,7 +95,7 @@
 
     fetches[1].wait()
     two = small_in[...].astype(jnp.float32)
-    my_line = small.at[pl.ds(block * OWNERS + odd_y * 2 + odd_x, 1)]
+    my_line = small.at[pl.ds((quarter * NZ + z) * OWNERS + far_y * 2 + far_x, 1)]
     my_line[...] = jnp.concatenate([two[0:1], two[1:2], two[0:1], two[1:2]], axis=1)
     fetches[2].wait()
     pair = ids_in[...]
@@ -111,7 +116,7 @@
     def _():
         pl.semaphore_wait(ready, 1)
         for side in FAR_SIDE[:-1]:
-            push(my_ring, my_ring, 0, ring_sem.at[0], mirror_peer(z, side, 1))
+            push(my_ring, my_ring, 0, ring_sem.at[0], near_peer(z, side, 1))
 
     for slot in range(1, OWNERS):
         push(my_line, my_line, 3, small_sem.at[0], gather_peer(slot, w))
@@ -127,10 +132,18 @@
             for core in (1, 0):
                 push(ring, bundle, 0, ids_sem.at[z], z_peer(kz, core))
         push(ring, bundle, 0, ids_sem.at[z], other)
+        pl.semaphore_signal(ready, inc=1, device_id=other, device_id_type=MESH)
         pltpu.make_async_copy(ring, bundle, ids_sem.at[z]).start()
 
+    @pl.when(w == 0)
+    def _():
+        pl.semaphore_wait(ready, 1)
+
     wait(small.at[pl.ds(0, OWNERS - 1)], small_sem.at[0])
-    my_block = small.at[pl.ds(block * OWNERS, OWNERS)]
+    my_block = small.at[pl.ds((quarter * NZ + z) * OWNERS, OWNERS)]
+    my_column = small.at[pl.ds(quarter * NZ * OWNERS, NZ * OWNERS)]
+    for kz in FAR_Z:
+        push(my_block, my_block, 3, small_sem.at[1], z_peer(kz, w))
 
     lane = lax.broadcasted_iota(jnp.int32, (1, 128), 1)
     low_half = lane < 64
@@ -139,16 +152,7 @@
 
     for plane in range(NZ):
         wait(ids.at[pl.ds(plane * SIDES, SIDES)], ids_sem.at[plane])
-        for side in FAR_SIDE:
-            if side:
-                push(my_block, my_block, 3, small_sem.at[1], mirror_peer(plane, side, w))
-                continue
-
-            @pl.when(plane != z)
-            def _():
-                push(my_block, my_block, 3, small_sem.at[1], mirror_peer(plane, side, w))
-
-        lines = [ids[pl.ds(plane * SIDES + mirror_line(side), 1), :] for side in range(SIDES)]
+        lines = [ids[pl.ds(plane * SIDES + near_line(side), 1), :] for side in range(SIDES)]
         wanted = jnp.concatenate(
             [jnp.where(low_half, a, b) for a, b in zip(lines[::2], lines[1::2])], axis=1
         )
@@ -178,21 +182,33 @@
         for side in FAR_SIDE:
             source, target = send.at[plane * SIDES + side], recv.at[block]
             if side:
-                push(source, target, 2, row_sem.at[0], mirror_peer(plane, side, w))
+                push(source, target, 2, row_sem.at[0], near_peer(plane, side, w))
                 continue
 
             @pl.when(plane != z)
             def _():
-                push(source, target, 2, row_sem.at[0], mirror_peer(plane, side, w))
+                push(source, target, 2, row_sem.at[0], near_peer(plane, side, w))
 
             @pl.when(plane == z)
             def _():
                 pltpu.make_async_copy(source, target, row_sem.at[0]).start()
 
-    wait(small.at[pl.ds(0, OWNERS * (PEERS - 1))], small_sem.at[1])
+        if plane < 3:
+            continue
+
+        @pl.when(jnp.maximum(z, 3) == plane)
+        def _():
+            wait(small.at[pl.ds(0, OWNERS * (NZ - 1))], small_sem.at[1])
+            for side in range(1, SIDES):
+                push(my_column, my_column, 3, small_sem.at[2], near_peer(z, side, w))
+
+    wait(small.at[pl.ds(0, OWNERS * NZ * (SIDES - 1))], small_sem.at[2])
     wanted = sid[...]
     device = wanted >> 1
-    line = (device & 0x79) | ((device & 2) << 1) | ((device & 4) >> 1)
+    high_bits = device >> 1
+    folded = device ^ high_bits
+    column = ((folded >> 1) & 2) | (folded & 1)
+    line = column * (NZ * OWNERS) + (device >> 4) * OWNERS + (((high_bits >> 1) & 2) | (high_bits & 1))
     lines = small[...].astype(jnp.bfloat16)
     small_rows = jnp.zeros((EX, F), jnp.float32)
     for row in range(2):
@@ -249,7 +265,7 @@
             pltpu.VMEM((PEERS, 16, 128), jnp.bfloat16),
             pltpu.VMEM((PEERS, 16, 128), jnp.bfloat16),
             pltpu.VMEM((OWNERS * PEERS, 128), jnp.float32),
-            dma((5,)), dma((4,)), dma((1,)), dma((1,)), dma((NZ,)), dma((1,)), dma((2,)),
+            dma((5,)), dma((4,)), dma((1,)), dma((1,)), dma((NZ,)), dma((1,)), dma((3,)),
             pltpu.SemaphoreType.REGULAR,
         ],
         compiler_params=pltpu.CompilerParams(

time: 22.8 us -> 21.4 us (0.939)
  the two profiles are of different devices: /device:TPU:225 before, /device:TPU:1 now
where the time goes in v8:
time: 21.4 us; the launch traced here: 21.3 us
  Pallas kernels  20.7 us (97%)
  local copies, waits for them, and re-layouts  0.61 us (3%)
    pallas_call x1, Pallas kernels, shards(): pl.pallas_call(kernel, out_shape=jax.ShapeDtypeStruct((3, EX, F), jnp.bfl...  20.7 us
    unnamed x1, local copies, waits for them, and re-layouts  0.61 us

profile of v8, /device:TPU:1, one launch (start us, length us, event | category | flops | bytes accessed | tf_op | source)
XLA Modules:
  0.0 21.3 jit_solution(7865549011859190810)
XLA Ops:
  0.0 20.7 %shard_map.55 = bf16[3,32,32]{2,1,0:T(8,128)(2,1)S(1)} custom-call(s32[2,32]{1,0:T(2,128)} %bitcast.6, bf16[32,1024]{1,0:T(8,128)(2,1)} %bitcast.5, f32[32,32]{1,0:T(8,128)} %dense_hbm.1, s32[1,32]{1,0:T(1,128)} %bitcast.7, bf16[2,32]{1,0:T(2,128)(2,1)} %small_hbm.1), custom_call_target="tpu_custom_call" | custom-call | tf_op jit(solution)/shard_map/pallas_call | solution.py:252
  20.7 0.6 %copy.7 = bf16[32,3,32]{2,0,1:T(8,128)(2,1)} copy(bf16[32,3,32]{2,0,1:T(8,128)(2,1)S(1)} %bitcast.4) | data formatting | bytes 12288

commit v9 on v8

--- a/solution.py
+++ b/solution.py
@@ -121,7 +121,7 @@
     for slot in range(1, OWNERS):
         push(my_line, my_line, 3, small_sem.at[0], gather_peer(slot, w))
     for slot in range(OWNERS - 1, 0, -1):
-        push(tab.at[0], tab.at[slot], 1, tab_sem.at[0], gather_peer(slot, w))
+        push(tab.at[0], tab.at[slot], 1, tab_sem.at[slot // 3], gather_peer(slot, w))
 
     @pl.when(w == 1)
     def _():
@@ -158,19 +158,22 @@
         )
         high = wanted >> 8
         hot = jnp.where(low_rows == (wanted & (LOW - 1)), 1.0, 0.0).astype(jnp.bfloat16)
-        if plane == 0:
-            wait(tab.at[pl.ds(1, OWNERS - 1)], tab_sem.at[0])
-        lhs = jnp.concatenate(
-            [tab[j, :, b * LOW : (b + 1) * LOW] for j in range(OWNERS) for b in range(HIGH)], axis=0
-        )
-        found = jnp.dot(lhs, hot, preferred_element_type=jnp.float32)
         rows = jnp.zeros((F, WIDE), jnp.float32)
-        for j in range(OWNERS):
-            yo, xo = owner(j)
-            for b in range(HIGH):
-                at = (j * HIGH + b) * F
-                here = ((z * NY + yo) * NX + xo) * HIGH + b
-                rows = jnp.where(high == here, found[at : at + F], rows)
+        for slots in ((0, 1, 2), (3,)) if plane == 0 else ((0, 1), (2, 3)):
+            if plane == 0:
+                first = max(slots[0], 1)
+                wait(tab.at[pl.ds(first, slots[-1] - first + 1)], tab_sem.at[first // 3])
+            lhs = jnp.concatenate(
+                [tab[j, :, b * LOW : (b + 1) * LOW] for j in slots for b in range(HIGH)], axis=0
+            )
+            found = jnp.dot(lhs, hot, preferred_element_type=jnp.float32)
+            at = 0
+            for j in slots:
+                yo, xo = owner(j)
+                for b in range(HIGH):
+                    here = ((z * NY + yo) * NX + xo) * HIGH + b
+                    rows = jnp.where(high == here, found[at : at + F], rows)
+                    at += F
         for half in range(SIDES // 2):
             part = rows[:, half * 128 : (half + 1) * 128]
             upper, lower = part[:16], part[16:]
@@ -202,6 +205,15 @@
             for side in range(1, SIDES):
                 push(my_column, my_column, 3, small_sem.at[2], near_peer(z, side, w))
 
+    @pl.when(w == 1)
+    def _():
+        wait(ids.at[pl.ds(0, PEERS)], send_sem.at[0])
+        wait(ids.at[pl.ds(0, PEERS - 1)], send_sem.at[0])
+
+    wait(tab.at[pl.ds(1, OWNERS - 1)], send_sem.at[1])
+    wait(small.at[pl.ds(0, OWNERS * PEERS - 1)], send_sem.at[3])
+    wait(send.at[pl.ds(1, PEERS - 1)], send_sem.at[2])
+    wait(recv.at[pl.ds(0, PEERS)], row_sem.at[0])
     wait(small.at[pl.ds(0, OWNERS * NZ * (SIDES - 1))], small_sem.at[2])
     wanted = sid[...]
     device = wanted >> 1
@@ -222,15 +234,6 @@
         )
     out_ref[2] = small_rows.astype(jnp.bfloat16)
 
-    @pl.when(w == 1)
-    def _():
-        wait(ids.at[pl.ds(0, PEERS)], send_sem.at[0])
-        wait(ids.at[pl.ds(0, PEERS - 1)], send_sem.at[0])
-
-    wait(tab.at[pl.ds(1, OWNERS - 1)], send_sem.at[1])
-    wait(small.at[pl.ds(0, OWNERS * PEERS - 1)], send_sem.at[3])
-    wait(send.at[pl.ds(1, PEERS - 1)], send_sem.at[2])
-    wait(recv.at[pl.ds(0, PEERS)], row_sem.at[0])
     total = recv[0].astype(jnp.float32)
     for slot in range(1, PEERS):
         total = total + recv[slot].astype(jnp.float32)
@@ -265,7 +268,7 @@
             pltpu.VMEM((PEERS, 16, 128), jnp.bfloat16),
             pltpu.VMEM((PEERS, 16, 128), jnp.bfloat16),
             pltpu.VMEM((OWNERS * PEERS, 128), jnp.float32),
-            dma((5,)), dma((4,)), dma((1,)), dma((1,)), dma((NZ,)), dma((1,)), dma((3,)),
+            dma((5,)), dma((4,)), dma((2,)), dma((1,)), dma((NZ,)), dma((1,)), dma((3,)),
             pltpu.SemaphoreType.REGULAR,
         ],
         compiler_params=pltpu.CompilerParams(

time: 21.4 us -> 21.3 us (level)
  no operation moved by 1% of the time
where the time goes in v9:
time: 21.3 us; the launch traced here: 21.2 us
  Pallas kernels  20.6 us (97%)
  local copies, waits for them, and re-layouts  0.61 us (3%)
    pallas_call x1, Pallas kernels, shards(): pl.pallas_call(kernel, out_shape=jax.ShapeDtypeStruct((3, EX, F), jnp.bfl...  20.6 us
    unnamed x1, local copies, waits for them, and re-layouts  0.61 us

profile of v9, /device:TPU:1, one launch (start us, length us, event | category | flops | bytes accessed | tf_op | source)
XLA Modules:
  0.0 21.2 jit_solution(13528228597175315092)
XLA Ops:
  0.0 20.6 %shard_map.55 = bf16[3,32,32]{2,1,0:T(8,128)(2,1)S(1)} custom-call(s32[2,32]{1,0:T(2,128)} %bitcast.6, bf16[32,1024]{1,0:T(8,128)(2,1)} %bitcast.5, f32[32,32]{1,0:T(8,128)} %dense_hbm.1, s32[1,32]{1,0:T(1,128)} %bitcast.7, bf16[2,32]{1,0:T(2,128)(2,1)} %small_hbm.1), custom_call_target="tpu_custom_call" | custom-call | tf_op jit(solution)/shard_map/pallas_call | solution.py:255
  20.6 0.6 %copy.7 = bf16[32,3,32]{2,0,1:T(8,128)(2,1)} copy(bf16[32,3,32]{2,0,1:T(8,128)(2,1)S(1)} %bitcast.4) | data formatting | bytes 12288

commit v10 on v9

--- a/solution.py
+++ b/solution.py
@@ -65,11 +65,8 @@
         pl.semaphore_signal(barrier, inc=1, device_id=gather_peer(slot, 0), device_id_type=MESH)
     pl.semaphore_signal(barrier, inc=1, device_id=other, device_id_type=MESH)
 
-    @pl.when(w == 1)
-    def _():
-        for side in range(1, SIDES):
-            peer = near_peer(z, side, 0)
-            pl.semaphore_signal(barrier, inc=1, device_id=peer, device_id_type=MESH)
+    for side in range(1, SIDES):
+        pl.semaphore_signal(barrier, inc=1, device_id=near_peer(z, side, 0), device_id_type=MESH)
 
 
     fetches = [
@@ -95,7 +92,8 @@
 
     fetches[1].wait()
     two = small_in[...].astype(jnp.float32)
-    my_line = small.at[pl.ds((quarter * NZ + z) * OWNERS + far_y * 2 + far_x, 1)]
+    far = far_y * 2 + far_x
+    my_line = small.at[pl.ds((far * NZ + z) * SIDES + quarter, 1)]
     my_line[...] = jnp.concatenate([two[0:1], two[1:2], two[0:1], two[1:2]], axis=1)
     fetches[2].wait()
     pair = ids_in[...]
@@ -109,7 +107,7 @@
 
     @pl.when(w == 0)
     def _():
-        pl.semaphore_wait(barrier, 2 * (OWNERS - 1) + SIDES)
+        pl.semaphore_wait(barrier, 2 * (OWNERS + SIDES - 2) + 1)
         pl.semaphore_signal(ready, inc=1, device_id=other, device_id_type=MESH)
 
     @pl.when(w == 1)
@@ -118,8 +116,8 @@
         for side in FAR_SIDE[:-1]:
             push(my_ring, my_ring, 0, ring_sem.at[0], near_peer(z, side, 1))
 
-    for slot in range(1, OWNERS):
-        push(my_line, my_line, 3, small_sem.at[0], gather_peer(slot, w))
+    for side in range(1, SIDES):
+        push(my_line, my_line, 3, small_sem.at[0], near_peer(z, side, w))
     for slot in range(OWNERS - 1, 0, -1):
         push(tab.at[0], tab.at[slot], 1, tab_sem.at[slot // 3], gather_peer(slot, w))
 
@@ -140,8 +138,8 @@
         pl.semaphore_wait(ready, 1)
 
     wait(small.at[pl.ds(0, OWNERS - 1)], small_sem.at[0])
-    my_block = small.at[pl.ds((quarter * NZ + z) * OWNERS, OWNERS)]
-    my_column = small.at[pl.ds(quarter * NZ * OWNERS, NZ * OWNERS)]
+    my_block = small.at[pl.ds((far * NZ + z) * SIDES, SIDES)]
+    my_column = small.at[pl.ds(far * NZ * SIDES, NZ * SIDES)]
     for kz in FAR_Z:
         push(my_block, my_block, 3, small_sem.at[1], z_peer(kz, w))
 
@@ -196,14 +194,10 @@
             def _():
                 pltpu.make_async_copy(source, target, row_sem.at[0]).start()
 
-        if plane < 3:
-            continue
-
-        @pl.when(jnp.maximum(z, 3) == plane)
-        def _():
+        if plane == 3:
             wait(small.at[pl.ds(0, OWNERS * (NZ - 1))], small_sem.at[1])
-            for side in range(1, SIDES):
-                push(my_column, my_column, 3, small_sem.at[2], near_peer(z, side, w))
+            for slot in range(1, OWNERS):
+                push(my_column, my_column, 3, small_sem.at[2], gather_peer(slot, w))
 
     @pl.when(w == 1)
     def _():
@@ -220,7 +214,7 @@
     high_bits = device >> 1
     folded = device ^ high_bits
     column = ((folded >> 1) & 2) | (folded & 1)
-    line = column * (NZ * OWNERS) + (device >> 4) * OWNERS + (((high_bits >> 1) & 2) | (high_bits & 1))
+    line = ((((high_bits >> 1) & 2) | (high_bits & 1)) * NZ + (device >> 4)) * SIDES + column
     lines = small[...].astype(jnp.bfloat16)
     small_rows = jnp.zeros((EX, F), jnp.float32)
     for row in range(2):

time: 21.3 us -> 21.1 us (level)
  Pallas kernels: 20.6 us -> 20.3 us
    pallas_call x1, Pallas kernels: 20.6 us -> 20.3 us  [shards(): pl.pallas_call(kernel, out_shape=jax.ShapeDtypeStruct((3, EX, F), jnp.bfl...]
where the time goes in v10:
time: 21.1 us; the launch traced here: 21 us
  Pallas kernels  20.3 us (96%)
  local copies, waits for them, and re-layouts  0.61 us (3%)
    pallas_call x1, Pallas kernels, shards(): pl.pallas_call(kernel, out_shape=jax.ShapeDtypeStruct((3, EX, F), jnp.bfl...  20.3 us
    unnamed x1, local copies, waits for them, and re-layouts  0.61 us

profile of v10, /device:TPU:1, one launch (start us, length us, event | category | flops | bytes accessed | tf_op | source)
XLA Modules:
  0.0 21.0 jit_solution(2184015192082554005)
XLA Ops:
  0.0 20.3 %shard_map.55 = bf16[3,32,32]{2,1,0:T(8,128)(2,1)S(1)} custom-call(s32[2,32]{1,0:T(2,128)} %bitcast.6, bf16[32,1024]{1,0:T(8,128)(2,1)} %bitcast.5, f32[32,32]{1,0:T(8,128)} %dense_hbm.1, s32[1,32]{1,0:T(1,128)} %bitcast.7, bf16[2,32]{1,0:T(2,128)(2,1)} %small_hbm.1), custom_call_target="tpu_custom_call" | custom-call | tf_op jit(solution)/shard_map/pallas_call | solution.py:249
  20.3 0.6 %copy.7 = bf16[32,3,32]{2,0,1:T(8,128)(2,1)} copy(bf16[32,3,32]{2,0,1:T(8,128)(2,1)S(1)} %bitcast.4) | data formatting | bytes 12288

commit v11 on v10

--- a/solution.py
+++ b/solution.py
@@ -38,6 +38,8 @@
         fy, fx = BLOCKS[slot]
         return NY - 1 - y if fy else y, NX - 1 - x if fx else x
 
+    part = z - z // 4 * (z - 4)
+
     def gather_peer(slot, core):
         return (z, *owner(slot), core)
 
@@ -128,10 +130,10 @@
         wait(ring.at[pl.ds(0, SIDES - 1)], ring_sem.at[0])
         for kz in FAR_Z:
             for core in (1, 0):
-                push(ring, bundle, 0, ids_sem.at[z], z_peer(kz, core))
-        push(ring, bundle, 0, ids_sem.at[z], other)
+                push(ring, bundle, 0, ids_sem.at[part], z_peer(kz, core))
+        push(ring, bundle, 0, ids_sem.at[part], other)
         pl.semaphore_signal(ready, inc=1, device_id=other, device_id_type=MESH)
-        pltpu.make_async_copy(ring, bundle, ids_sem.at[z]).start()
+        pltpu.make_async_copy(ring, bundle, ids_sem.at[part]).start()
 
     @pl.when(w == 0)
     def _():
@@ -149,7 +151,9 @@
     low_rows = lax.broadcasted_iota(jnp.int32, (LOW, WIDE), 0)
 
     for plane in range(NZ):
-        wait(ids.at[pl.ds(plane * SIDES, SIDES)], ids_sem.at[plane])
+        if plane <= 4:
+            planes = 1 if plane < 4 else NZ - 4
+            wait(ids.at[pl.ds(plane * SIDES, planes * SIDES)], ids_sem.at[plane])
         lines = [ids[pl.ds(plane * SIDES + near_line(side), 1), :] for side in range(SIDES)]
         wanted = jnp.concatenate(
             [jnp.where(low_half, a, b) for a, b in zip(lines[::2], lines[1::2])], axis=1
@@ -262,7 +266,7 @@
             pltpu.VMEM((PEERS, 16, 128), jnp.bfloat16),
             pltpu.VMEM((PEERS, 16, 128), jnp.bfloat16),
             pltpu.VMEM((OWNERS * PEERS, 128), jnp.float32),
-            dma((5,)), dma((4,)), dma((2,)), dma((1,)), dma((NZ,)), dma((1,)), dma((3,)),
+            dma((5,)), dma((4,)), dma((2,)), dma((1,)), dma((5,)), dma((1,)), dma((3,)),
             pltpu.SemaphoreType.REGULAR,
         ],
         compiler_params=pltpu.CompilerParams(

time: 21.1 us -> 21 us (level)
  no operation moved by 1% of the time
where the time goes in v11:
time: 21 us; the launch traced here: 20.9 us
  Pallas kernels  20.3 us (97%)
  local copies, waits for them, and re-layouts  0.61 us (3%)
    pallas_call x1, Pallas kernels, shards(): pl.pallas_call(kernel, out_shape=jax.ShapeDtypeStruct((3, EX, F), jnp.bfl...  20.3 us
    unnamed x1, local copies, waits for them, and re-layouts  0.61 us

profile of v11, /device:TPU:1, one launch (start us, length us, event | category | flops | bytes accessed | tf_op | source)
XLA Modules:
  0.0 20.9 jit_solution(6571706828879705280)
XLA Ops:
  0.0 20.3 %shard_map.55 = bf16[3,32,32]{2,1,0:T(8,128)(2,1)S(1)} custom-call(s32[2,32]{1,0:T(2,128)} %bitcast.6, bf16[32,1024]{1,0:T(8,128)(2,1)} %bitcast.5, f32[32,32]{1,0:T(8,128)} %dense_hbm.1, s32[1,32]{1,0:T(1,128)} %bitcast.7, bf16[2,32]{1,0:T(2,128)(2,1)} %small_hbm.1), custom_call_target="tpu_custom_call" | custom-call | tf_op jit(solution)/shard_map/pallas_call | solution.py:253
  20.3 0.6 %copy.7 = bf16[32,3,32]{2,0,1:T(8,128)(2,1)} copy(bf16[32,3,32]{2,0,1:T(8,128)(2,1)S(1)} %bitcast.4) | data formatting | bytes 12288

commit v12 on v10

--- a/solution.py
+++ b/solution.py
@@ -228,9 +228,10 @@
         )
     out_ref[2] = small_rows.astype(jnp.bfloat16)
 
-    total = recv[0].astype(jnp.float32)
-    for slot in range(1, PEERS):
-        total = total + recv[slot].astype(jnp.float32)
+    blocks = [recv[slot] for slot in range(PEERS)]
+    while len(blocks) > 1:
+        blocks = [a + b for a, b in zip(blocks[::2], blocks[1::2])]
+    total = blocks[0].astype(jnp.float32)
     both = jnp.concatenate(
         [jnp.where(low_half16, total, 0.0), jnp.where(low_half16, 0.0, total)], axis=0
     ).astype(jnp.bfloat16)

time: 21.1 us -> 21.1 us (level)
  no operation moved by 1% of the time
where the time goes in v12:
time: 21.1 us; the launch traced here: 21 us
  Pallas kernels  20.3 us (96%)
  local copies, waits for them, and re-layouts  0.61 us (3%)
    pallas_call x1, Pallas kernels, shards(): pl.pallas_call(kernel, out_shape=jax.ShapeDtypeStruct((3, EX, F), jnp.bfl...  20.3 us
    unnamed x1, local copies, waits for them, and re-layouts  0.61 us

profile of v12, /device:TPU:1, one launch (start us, length us, event | category | flops | bytes accessed | tf_op | source)
XLA Modules:
  0.0 21.0 jit_solution(14276335657085002680)
XLA Ops:
  0.0 20.3 %shard_map.55 = bf16[3,32,32]{2,1,0:T(8,128)(2,1)S(1)} custom-call(s32[2,32]{1,0:T(2,128)} %bitcast.6, bf16[32,1024]{1,0:T(8,128)(2,1)} %bitcast.5, f32[32,32]{1,0:T(8,128)} %dense_hbm.1, s32[1,32]{1,0:T(1,128)} %bitcast.7, bf16[2,32]{1,0:T(2,128)(2,1)} %small_hbm.1), custom_call_target="tpu_custom_call" | custom-call | tf_op jit(solution)/shard_map/pallas_call | solution.py:250
  20.4 0.6 %copy.7 = bf16[32,3,32]{2,0,1:T(8,128)(2,1)} copy(bf16[32,3,32]{2,0,1:T(8,128)(2,1)S(1)} %bitcast.4) | data formatting | bytes 12288

commit v13 on v11

--- a/solution.py
+++ b/solution.py
@@ -61,15 +61,14 @@
 
     barrier = pltpu.get_barrier_semaphore()
     other = (z, y, x, 1 - w)
-    for kz in FAR_Z:
-        pl.semaphore_signal(barrier, inc=1, device_id=z_peer(kz, 1), device_id_type=MESH)
     for slot in range(1, OWNERS):
         pl.semaphore_signal(barrier, inc=1, device_id=gather_peer(slot, 0), device_id_type=MESH)
     pl.semaphore_signal(barrier, inc=1, device_id=other, device_id_type=MESH)
 
     for side in range(1, SIDES):
         pl.semaphore_signal(barrier, inc=1, device_id=near_peer(z, side, 0), device_id_type=MESH)
-
+    for kz in FAR_Z:
+        pl.semaphore_signal(barrier, inc=1, device_id=z_peer(kz, 1), device_id_type=MESH)
 
     fetches = [
         pltpu.make_async_copy(src, dst, local_sem.at[i])
@@ -232,9 +231,10 @@
         )
     out_ref[2] = small_rows.astype(jnp.bfloat16)
 
-    total = recv[0].astype(jnp.float32)
-    for slot in range(1, PEERS):
-        total = total + recv[slot].astype(jnp.float32)
+    blocks = [recv[slot] for slot in range(PEERS)]
+    while len(blocks) > 1:
+        blocks = [a + b for a, b in zip(blocks[::2], blocks[1::2])]
+    total = blocks[0].astype(jnp.float32)
     both = jnp.concatenate(
         [jnp.where(low_half16, total, 0.0), jnp.where(low_half16, 0.0, total)], axis=0
     ).astype(jnp.bfloat16)

time: 21 us -> 21 us (level)
  no operation moved by 1% of the time
where the time goes in v13:
time: 21 us; the launch traced here: 20.9 us
  Pallas kernels  20.3 us (97%)
  local copies, waits for them, and re-layouts  0.61 us (3%)
    pallas_call x1, Pallas kernels, shards(): pl.pallas_call(kernel, out_shape=jax.ShapeDtypeStruct((3, EX, F), jnp.bfl...  20.3 us
    unnamed x1, local copies, waits for them, and re-layouts  0.61 us

profile of v13, /device:TPU:1, one launch (start us, length us, event | category | flops | bytes accessed | tf_op | source)
XLA Modules:
  0.0 20.9 jit_solution(16704704485095130948)
XLA Ops:
  0.0 20.3 %shard_map.55 = bf16[3,32,32]{2,1,0:T(8,128)(2,1)S(1)} custom-call(s32[2,32]{1,0:T(2,128)} %bitcast.6, bf16[32,1024]{1,0:T(8,128)(2,1)} %bitcast.5, f32[32,32]{1,0:T(8,128)} %dense_hbm.1, s32[1,32]{1,0:T(1,128)} %bitcast.7, bf16[2,32]{1,0:T(2,128)(2,1)} %small_hbm.1), custom_call_target="tpu_custom_call" | custom-call | tf_op jit(solution)/shard_map/pallas_call | solution.py:253
  20.3 0.6 %copy.7 = bf16[32,3,32]{2,0,1:T(8,128)(2,1)} copy(bf16[32,3,32]{2,0,1:T(8,128)(2,1)S(1)} %bitcast.4) | data formatting | bytes 12288

commit v14 on v10

--- a/solution.py
+++ b/solution.py
@@ -116,10 +116,10 @@
         for side in FAR_SIDE[:-1]:
             push(my_ring, my_ring, 0, ring_sem.at[0], near_peer(z, side, 1))
 
+    for slot in range(OWNERS - 1, 0, -1):
+        push(tab.at[0], tab.at[slot], 1, tab_sem.at[slot // 3], gather_peer(slot, w))
     for side in range(1, SIDES):
         push(my_line, my_line, 3, small_sem.at[0], near_peer(z, side, w))
-    for slot in range(OWNERS - 1, 0, -1):
-        push(tab.at[0], tab.at[slot], 1, tab_sem.at[slot // 3], gather_peer(slot, w))
 
     @pl.when(w == 1)
     def _():

time: 21.1 us -> 21.1 us (level)
  no operation moved by 1% of the time
where the time goes in v14:
time: 21.1 us; the launch traced here: 21 us
  Pallas kernels  20.3 us (96%)
  local copies, waits for them, and re-layouts  0.61 us (3%)
    pallas_call x1, Pallas kernels, shards(): pl.pallas_call(kernel, out_shape=jax.ShapeDtypeStruct((3, EX, F), jnp.bfl...  20.3 us
    unnamed x1, local copies, waits for them, and re-layouts  0.61 us

profile of v14, /device:TPU:1, one launch (start us, length us, event | category | flops | bytes accessed | tf_op | source)
XLA Modules:
  0.0 21.0 jit_solution(12413496369650727875)
XLA Ops:
  0.0 20.3 %shard_map.55 = bf16[3,32,32]{2,1,0:T(8,128)(2,1)S(1)} custom-call(s32[2,32]{1,0:T(2,128)} %bitcast.6, bf16[32,1024]{1,0:T(8,128)(2,1)} %bitcast.5, f32[32,32]{1,0:T(8,128)} %dense_hbm.1, s32[1,32]{1,0:T(1,128)} %bitcast.7, bf16[2,32]{1,0:T(2,128)(2,1)} %small_hbm.1), custom_call_target="tpu_custom_call" | custom-call | tf_op jit(solution)/shard_map/pallas_call | solution.py:249
  20.3 0.6 %copy.7 = bf16[32,3,32]{2,0,1:T(8,128)(2,1)} copy(bf16[32,3,32]{2,0,1:T(8,128)(2,1)S(1)} %bitcast.4) | data formatting | bytes 12288
